TPU v7x, 128 devices: a whole 4x4x4 slice. The times are simulated.
128 devices in a mesh: grp: 4 (over z), seq: 32 (over x, y, core).
Axes of the slice: x: 4, y: 4, z: 4, core: 2. Of those that a mesh axis runs over, the one named last changes fastest.
Arguments:
- latent: bfloat16 [4, 4096, 32, 256], P('grp', 'seq'), may hold values from -6 to 6
- up_key: bfloat16 [4, 128, 256], replicated, may hold values from -0.5 to 0.5
- up_value: bfloat16 [4, 128, 256], replicated, may hold values from -0.5 to 0.5
- queries: bfloat16 [8, 64, 128], replicated, may hold values from -240 to 240, as said below
- lengths: int32 [8], replicated, may hold values from 1 to 16384
- block_dest: int32 [4096], replicated, may hold values from 0 to 127, as said below
Outputs:
- decode_latent: bfloat16 [128, 4, 32, 32, 256], P(('grp', 'seq'))
- attended: float32 [8, 8192], replicated
Inputs may be any that keep to these rules, and one draw needn't show every extreme that they name: `block_dest`: each aligned run of 128 entries (the blocks of one seq index in the prefill layout) names every decode device exactly once. `queries`: the new token's query entries, real-valued.
All inputs are finite; a program needn't handle non-finite values.
Results may differ from a plain program's by a relative error of at most 0.001.
Values may be sent and summed in bfloat16 or wider, within the bound.
No kernel may reach another device: no remote copies, remote signals or barrier semaphores. Data moves between devices by JAX's collectives and lax.ppermute only.
A program may use at most 64 MiB of HBM per device.

v0:
```python
import jax
import jax.numpy as jnp
from jax import lax
from jax.sharding import Mesh
from jax.sharding import PartitionSpec as P

SEQ = ("seq_0", "seq_1", "seq_2")
GRP_SEQ = ("grp", "seq_0", "seq_1", "seq_2")


def all_in_one(x, axis):
    leaves = jax.tree.leaves(x)
    turns = sorted(range(len(leaves)), key=lambda k: -leaves[k].size)
    width = (1, *leaves[turns[0]].shape)[-1]
    lines = [
        jnp.pad(leaves[k].reshape(-1), (0, -leaves[k].size % width)).reshape(-1, width)
        for k in turns
    ]
    both, at, found = (lax.all_gather(jnp.concatenate(lines), axis), 0, {})
    for k, line in zip(turns, lines):
        slab = both[:, at : at + len(line)].reshape(len(both), -1)
        found[k] = slab[:, : leaves[k].size].reshape(-1, *leaves[k].shape)
        at += len(line)
    numbers = iter(range(len(leaves)))
    return jax.tree.map(lambda _: found[next(numbers)], x)


def joined_all(x, axes, combine):
    for axis in axes:
        pieces = all_in_one(x, axis)
        x = jax.tree.map(lambda part: part[0], pieces)
        for k in range(1, lax.axis_size(axis)):
            x = combine(x, jax.tree.map(lambda part: part[k], pieces))
    return x


def combine(first, second):
    largest = jnp.maximum(first[0], second[0])
    factor_a = jnp.exp(first[0] - largest)
    factor_b = jnp.exp(second[0] - largest)
    totals = first[1] * factor_a + second[1] * factor_b
    accum = first[2] * factor_a[..., None] + second[2] * factor_b[..., None]
    return (largest, totals, accum)


def slot_info(global_ids, lengths, block_len, blk_seq, batch):
    seq_ids = global_ids // blk_seq
    starts = global_ids % blk_seq * block_len
    positions = starts[:, None] + jnp.arange(block_len, dtype=jnp.int32)[None, :]
    seq_hot = (seq_ids[:, None] == jnp.arange(batch, dtype=jnp.int32)[None, :]).astype(jnp.int32)
    slot_len = jnp.sum(seq_hot * lengths[None, :], axis=1)
    live = positions < slot_len[:, None]
    return (seq_hot, live)


def partials(cache, key_map, value_map, slot_query, live, seq_hot):
    rank = cache.shape[3] // 2
    head_dim = slot_query.shape[-1]
    scale = 1.0 / float(head_dim) ** 0.5
    highest = lax.Precision.HIGHEST
    key_lat = cache[..., :rank]
    value_lat = cache[..., rank:]
    keys = jnp.einsum("gstr,grkd->gstkd", key_lat, key_map, preferred_element_type=jnp.float32)
    scores = (
        jnp.einsum("gstkd,sgkjd->gskjt", keys, slot_query.astype(jnp.float32), precision=highest)
        * scale
    )
    live_wide = live[None, :, None, None, :]
    scores = jnp.where(live_wide, scores, -1e30)
    slot_max = jnp.max(scores, axis=-1)
    weights = jnp.where(live_wide, jnp.exp(scores - slot_max[..., None]), 0.0)
    slot_tot = jnp.sum(weights, axis=-1)
    values = jnp.einsum(
        "gstr,grkd->gstkd", value_lat, value_map, preferred_element_type=jnp.float32
    )
    slot_acc = jnp.einsum("gskjt,gstkd->gskjd", weights, values, precision=highest)
    hot_bool = seq_hot > 0
    hot_float = seq_hot.astype(jnp.float32)
    spread = jnp.where(hot_bool[None, :, None, None, :], slot_max[..., None], -1e30)
    seq_max = jnp.max(spread, axis=1)
    slot_seq_max = jnp.sum(
        jnp.where(hot_bool[None, :, None, None, :], seq_max[:, None], 0.0), axis=-1
    )
    factor = jnp.exp(slot_max - slot_seq_max)
    totals = jnp.einsum("gskj,sb->gkjb", slot_tot * factor, hot_float, precision=highest)
    accum = jnp.einsum(
        "gskjd,sb->gkjbd", slot_acc * factor[..., None], hot_float, precision=highest
    )
    return (seq_max, totals, accum)


def body(latent, up_key, up_value, queries, lengths, block_dest):
    groups = up_key.shape[0]
    dests = latent.shape[1]
    block_len = latent.shape[2]
    rank = latent.shape[3] // 2
    shards = block_dest.shape[0] // dests
    batch = queries.shape[0]
    q_heads = queries.shape[1]
    head_dim = queries.shape[2]
    per_group = up_key.shape[2] // head_dim
    per_kv = q_heads // (groups * per_group)
    blk_seq = block_dest.shape[0] // batch
    own_shard = lax.axis_index(SEQ)
    own_dests = lax.dynamic_slice_in_dim(block_dest, own_shard * dests, dests)
    source_order = (
        jnp.zeros((dests,), jnp.int32).at[own_dests].set(jnp.arange(dests, dtype=jnp.int32))
    )
    outgoing = latent[0][source_order]
    received = lax.all_to_all(outgoing, GRP_SEQ, split_axis=0, concat_axis=0, tiled=True)
    received = received.reshape(groups, shards, block_len, 2 * rank)
    decode_latent = received[None]
    key_map = up_key.reshape(groups, rank, per_group, head_dim)
    value_map = up_value.reshape(groups, rank, per_group, head_dim)
    query_rows = queries.reshape(batch, q_heads * head_dim)
    own_group = lax.axis_index("grp")
    slots = latent.shape[1]
    global_ids = own_shard * slots + jnp.arange(slots, dtype=jnp.int32)
    seq_hot, live = slot_info(global_ids, lengths, block_len, blk_seq, batch)
    picked = jnp.dot(seq_hot.astype(jnp.bfloat16), query_rows, preferred_element_type=jnp.float32)
    slot_query = picked.astype(jnp.bfloat16).reshape(slots, groups, per_group, per_kv, head_dim)
    group_query = lax.dynamic_slice_in_dim(slot_query, own_group, 1, 1)
    group_key = lax.dynamic_slice_in_dim(key_map, own_group, 1, 0)
    group_value = lax.dynamic_slice_in_dim(value_map, own_group, 1, 0)
    local = partials(latent, group_key, group_value, group_query, live, seq_hot)
    merged = joined_all(local, SEQ, combine)
    part_result = merged[2] / merged[1][..., None]
    result = lax.all_gather(part_result, "grp", axis=0, tiled=True)
    attended = jnp.transpose(result, (3, 0, 1, 2, 4)).reshape(batch, q_heads * head_dim)
    return (decode_latent, attended)


def solution(mesh):
    finer = Mesh(
        mesh.devices.reshape(mesh.shape["grp"], 4, 4, 2), ("grp", "seq_0", "seq_1", "seq_2")
    )
    in_specs = (P("grp", SEQ, None, None), P(), P(), P(), P(), P())
    out_specs = (P(GRP_SEQ, None, None, None, None), P())
    return jax.shard_map(body, mesh=finer, in_specs=in_specs, out_specs=out_specs, check_vma=False)
```

profile of v0, /device:TPU:0, one launch (start us, length us, event | category | flops | bytes accessed | tf_op | source)
XLA Modules:
  0.0 82.2 jit_solution(2277621008148799493)
XLA Ops:
  0.6 0.8 compare_select_fusion.1
  1.4 1.0 %scatter_custom_fusion = s32[128]{0:T(128)S(1)} fusion(s32[128]{0:T(128)S(1)} %compare_select_fusion.1, s32[128]{0:T(128)S(1)} %iota.27, s32[]{:T(128)} %constant.26.clone.1), kind=kCustom, calls=%fused_computation.172 | custom fusion | bytes 516 | tf_op jit(solution)/shard_map/scatter | solution.py:107
  2.4 3.6 %gather_fusion = bf16[128,32,256]{2,1,0:T(8,128)(2,1)} fusion(bf16[128,32,256]{2,1,0:T(8,128)(2,1)} %bitcast.358, s32[1024]{0:T(1024)S(1)} %pad_clamp_fusion), kind=kCustom, calls=%fused_computation | custom fusion | bytes 4194816 | tf_op jit(solution)/shard_map/gather | solution.py:109
  6.0 11.7 %all-to-all-start = ((bf16[128,32,256]{2,1,0:T(8,128)(2,1)}), bf16[128,32,256]{2,1,0:T(8,128)(2,1)}, u32[]{:S(2)}, u32[]{:S(2)}) async-start(bf16[128,32,256]{2,1,0:T(8,128)(2,1)} %gather_fusion), calls=%async_computation | async-start | bytes 4194304 | tf_op jit(solution)/shard_map/all_to_all | solution.py:110
  17.8 0.1 select_reduce_fusion.2
  18.0 0.1 constant_dynamic-slice_fusion
  18.1 0.7 fusion.14
  18.8 0.2 copy-done.3
  19.0 0.7 fusion.4
  19.8 0.6 copy.35
  20.4 0.1 add_compare_fusion
  20.5 3.6 %fusion.102 = (f32[128,2,8]{2,1,0:T(2,128)S(1)}, f32[128,2,8,32]{3,2,1,0:T(8,128)S(1)}) fusion(f32[2,128,128,32]{1,3,0,2:T(8,128)S(1)} %fusion.14, bf16[128,4,2,8,128]{4,3,2,1,0:T(8,128)(2,1)S(1)} %bitcast.359, s32[]{:T(128)S(6)} %select_n.72, pred[128,32]{1,0:T(8,128)(4,1)S(1)} %add_compare_fusion), kind=kOutput, calls=%fused_computation.176 | convolution fusion | flops 100857856 | bytes 5005316 | tf_op jit(solution)/shard_map/gstkd,sgkjd->gskjt/dot_general | solution.py:65
  24.2 0.1 select_reduce_fusion.1
  24.3 0.1 select_reduce_fusion
  24.5 0.1 copy.26
  24.7 0.7 convolution_bitcast_fusion
  25.4 0.8 fusion.21
  26.2 3.7 %fusion.5 = f32[128,2,8,128]{3,2,1,0:T(8,128)S(1)} fusion(f32[128,32,2,128]{3,1,0,2:T(8,128)S(1)} %convolution_bitcast_fusion, f32[128,2,8,32]{3,2,1,0:T(8,128)S(1)} %get-tuple-element.30, f32[128,2,8]{2,1,0:T(2,128)S(1)} %copy.26, f32[128,2,8]{2,1,0:T(2,128)S(1)} %get-tuple-element.29, pred[128,32]{1,0:T(8,128)(4,1)S(1)} %add_compare_fusion), kind=kOutput, calls=%fused_computation.9 | convolution fusion | flops 101056512 | bytes 5525504 | tf_op jit(solution)/shard_map/gskjt,gstkd->gskjd/dot_general | solution.py:76
  29.9 0.9 %fusion.17 = f32[8,2,8,128]{3,0,2,1:T(8,128)S(1)} fusion(f32[128,2,8,128]{3,2,1,0:T(8,128)S(1)} %fusion.5, s32[128]{0:T(128)S(1)} %get-tuple-element.31), kind=kOutput, calls=%fused_computation.15 | convolution fusion | flops 25168896 | bytes 1114624 | tf_op jit(solution)/shard_map/gskjd,sb->gkjbd/dot_general | solution.py:86
  30.8 0.1 fusion.49
  30.9 0.1 reshape.1167
  31.1 18.3 %all-gather.3 = f32[4,130,128]{2,1,0:T(8,128)S(1)} all-gather(f32[1,130,128]{2,1,0:T(8,128)S(1)} %maximum_bitcast_fusion), channel_id=2, replica_groups=mesh['grp'=4,'seq_0'=4,'seq_1'=4,'seq_2'=2] {'seq_0'}, dimensions={0}, use_global_device_ids=true | all-gather | bytes 332800 | tf_op jit(solution)/shard_map/all_gather | solution.py:19
  49.4 0.2 fusion.39
  49.6 12.7 %all-gather.4 = f32[4,130,128]{2,1,0:T(8,128)S(1)} all-gather(f32[1,130,128]{2,1,0:T(8,128)S(1)} %maximum_bitcast_fusion.1), channel_id=3, replica_groups=mesh['grp'=4,'seq_0'=4,'seq_1'=4,'seq_2'=2] {'seq_1'}, dimensions={0}, use_global_device_ids=true | all-gather | bytes 332800 | tf_op jit(solution)/shard_map/all_gather | solution.py:19
  62.4 0.2 fusion.30
  62.6 1.9 %all-gather.5 = f32[2,130,128]{2,1,0:T(8,128)S(1)} all-gather(f32[1,130,128]{2,1,0:T(8,128)S(1)} %maximum_bitcast_fusion.2), channel_id=4, replica_groups=mesh['grp'=4,'seq_0'=4,'seq_1'=4,'seq_2'=2] {'seq_2'}, dimensions={0}, use_global_device_ids=true | all-gather | bytes 199680 | tf_op jit(solution)/shard_map/all_gather | solution.py:19
  64.7 0.1 squeeze.146
  64.8 0.1 squeeze.147
  64.9 0.1 add_divide_fusion
  65.0 13.4 %all_gather.27 = f32[4,2,8,8,128]{4,3,2,1,0:T(8,128)S(1)} all-gather(f32[1,2,8,8,128]{4,3,2,1,0:T(8,128)S(1)} %add_divide_fusion), channel_id=1, replica_groups=mesh['grp'=4,'seq_0'=4,'seq_1'=4,'seq_2'=2] {'grp'}, dimensions={0}, use_global_device_ids=true | all-gather | bytes 327680 | tf_op jit(solution)/shard_map/all_gather | solution.py:128
  78.4 3.1 %copy.52 = bf16[1,4,32,32,256]{4,3,2,1,0:T(8,128)(2,1)} copy(bf16[1,4,32,32,256]{4,3,2,1,0:T(8,128)(2,1)} %bitcast.1) | data formatting | bytes 4194304
  81.5 0.7 copy.53
  (35 shorter events, 0.7 us)
Async XLA Ops:
  6.0 11.8 %copy-start.4 = (s32[8]{0:T(128)S(1)}, s32[8]{0:T(128)}, u32[]{:S(2)}) copy-start(s32[8]{0:T(128)} %param.10) | copy-start | bytes 100
  6.0 11.9 %copy-start.1 = (bf16[4,128,256]{2,1,0:T(8,128)(2,1)S(1)}, bf16[4,128,256]{2,1,0:T(8,128)(2,1)}, u32[]{:S(2)}) copy-start(bf16[4,128,256]{2,1,0:T(8,128)(2,1)} %param.7) | copy-start | bytes 786436
  6.0 11.9 %copy-start.2 = (bf16[4,128,256]{2,1,0:T(8,128)(2,1)S(1)}, bf16[4,128,256]{2,1,0:T(8,128)(2,1)}, u32[]{:S(2)}) copy-start(bf16[4,128,256]{2,1,0:T(8,128)(2,1)} %param.8) | copy-start | bytes 786436
  6.0 12.1 %copy-start = (bf16[1,128,32,256]{3,2,1,0:T(8,128)(2,1)S(1)}, bf16[1,128,32,256]{3,2,1,0:T(8,128)(2,1)}, u32[]{:S(2)}) copy-start(bf16[1,128,32,256]{3,2,1,0:T(8,128)(2,1)} %param.6) | copy-start | bytes 6291460
  6.0 72.4 %all-to-all-start = ((bf16[128,32,256]{2,1,0:T(8,128)(2,1)}), bf16[128,32,256]{2,1,0:T(8,128)(2,1)}, u32[]{:S(2)}, u32[]{:S(2)}) async-start(bf16[128,32,256]{2,1,0:T(8,128)(2,1)} %gather_fusion), calls=%async_computation | async-start | bytes 4194304 | tf_op jit(solution)/shard_map/all_to_all | solution.py:110
  18.1 0.9 %copy-start.3 = (bf16[8,64,128]{2,1,0:T(8,128)(2,1)S(1)}, bf16[8,64,128]{2,1,0:T(8,128)(2,1)}, u32[]{:S(2)}) copy-start(bf16[8,64,128]{2,1,0:T(8,128)(2,1)} %param.9) | copy-start | bytes 393220
where the time goes:
time: 82.5 us; the launch traced here: 82.2 us
  blocking collectives  46.3 us (56%)
  starting transfers between devices  11.7 us (14%)
  matrix products  10.4 us (13%)
  local copies, waits for them, and re-layouts  10.2 us (12%)
  other arithmetic  2.58 us (3%)
  between operations  0.89 us (1%)
    all_gather x3, blocking collectives, all_in_one(): both, at, found = (lax.all_gather(jnp.concatenate(lines), axis), 0, {})  32.9 us
    all_gather x1, blocking collectives, body(): result = lax.all_gather(part_result, 'grp', axis=0, tiled=True)  13.4 us
    all_to_all x1, starting transfers between devices, body(): lax.all_to_all(outgoing, GRP_SEQ, split_axis=0, concat_axis=0, tiled=True)  11.7 us
    unnamed x13, local copies, waits for them, and re-layouts  4.61 us
    dot_general x1, matrix products, partials(): jnp.einsum('gskjt,gstkd->gskjd', weights, values, precision=highest)  3.68 us
    dot_general x1, matrix products, partials(): jnp.einsum('gstkd,sgkjd->gskjt', keys, slot_query.astype(jnp.float32), pr...  3.63 us
    gather x1, local copies, waits for them, and re-layouts, body(): outgoing = latent[0][source_order]  3.59 us
  transfers between devices with their start and end apart: 1, of which 0 were waited for; matrix products, arithmetic and copies ran while one was open for 17% of the time, Pallas kernels for 0%

commit v1 on v0

v1 whole, which is shorter than its diff:
```python
import jax
import jax.numpy as jnp
from jax import lax
from jax.experimental import pallas as pl
from jax.experimental.pallas import tpu as pltpu
from jax.sharding import Mesh
from jax.sharding import PartitionSpec as P

SEQ = ("seq_0", "seq_1", "seq_2")
GRP_SEQ = ("grp", "seq_0", "seq_1", "seq_2")
NEG = -1e30


def slot_kernel(dests, latent, out, table, sem, sems):
    count = latent.shape[0]
    shard = lax.axis_index(SEQ)
    first = pltpu.make_async_copy(dests.at[pl.ds(shard * count, count)], table, sem)
    first.start()
    first.wait()

    def send(b, carry):
        pltpu.make_async_copy(latent.at[b], out.at[table[b]], sems).start()
        return carry

    lax.fori_loop(0, count, send, 0, unroll=8)
    pltpu.make_async_copy(latent, out, sems).wait()


def slotted(latent, dests):
    count = latent.shape[0]
    return pl.pallas_call(
        slot_kernel,
        out_shape=jax.ShapeDtypeStruct(latent.shape, latent.dtype),
        in_specs=[pl.BlockSpec(memory_space=pl.ANY), pl.BlockSpec(memory_space=pl.ANY)],
        out_specs=pl.BlockSpec(memory_space=pl.ANY),
        scratch_shapes=[
            pltpu.SMEM((count,), jnp.int32),
            pltpu.SemaphoreType.DMA,
            pltpu.SemaphoreType.DMA,
        ],
        name="slot",
    )(dests, latent)


def split(x, parts):
    pieces = []
    for _ in range(parts):
        piece = x.astype(jnp.bfloat16)
        pieces.append(piece)
        x = x - piece.astype(jnp.float32)
    return pieces


def attend_kernel(lengths, latent, up_key, queries, out):
    blocks, block_len, width = latent.shape
    rank = width // 2
    tokens = blocks * block_len
    heads = out.shape[1]
    head_dim = queries.shape[2]
    per_group = up_key.shape[2] // head_dim
    per_kv = heads // per_group
    shard = lax.axis_index(SEQ)
    group = lax.axis_index("grp")
    quarter = lax.axis_size(SEQ) // queries.shape[0]
    seq = shard // quarter
    live_count = lengths[seq] - (shard % quarter) * tokens
    query = queries[seq, pl.ds(pl.multiple_of(group * heads, heads), heads), :]
    query = query.astype(jnp.float32)
    key_map = up_key[group].astype(jnp.float32)
    rows = []
    for k in range(per_group):
        rows.append(
            lax.dot_general(
                query[k * per_kv : (k + 1) * per_kv].astype(jnp.bfloat16),
                key_map[:, k * head_dim : (k + 1) * head_dim].astype(jnp.bfloat16),
                (((1,), (1,)), ((), ())),
                preferred_element_type=jnp.float32,
            )
        )
    absorbed = jnp.concatenate(rows, axis=0) * (1.0 / float(head_dim) ** 0.5)
    lat = latent[...].reshape(tokens, width)
    parts = jnp.concatenate([p.astype(jnp.float32) for p in split(absorbed, 3)], axis=0)
    raw = lax.dot_general(
        parts.astype(jnp.bfloat16),
        lat[:, :rank],
        (((1,), (1,)), ((), ())),
        preferred_element_type=jnp.float32,
    )
    scores = raw[2 * heads :] + raw[heads : 2 * heads] + raw[:heads]
    live = lax.broadcasted_iota(jnp.int32, (heads, tokens), 1) < live_count
    scores = jnp.where(live, scores, NEG)
    largest = jnp.max(scores, axis=1, keepdims=True)
    weights = jnp.where(live, jnp.exp(scores - largest), 0.0)
    total = jnp.sum(weights, axis=1, keepdims=True)
    halves = jnp.concatenate([p.astype(jnp.float32) for p in split(weights, 2)], axis=0)
    summed = lax.dot_general(
        halves.astype(jnp.bfloat16),
        lat[:, rank:],
        (((1,), (0,)), ((), ())),
        preferred_element_type=jnp.float32,
    )
    out[0] = summed[:heads] + summed[heads:]
    out[1] = jnp.broadcast_to(largest, (heads, rank))
    out[2] = jnp.broadcast_to(total, (heads, rank))


def attend(latent, up_key, queries, lengths, heads):
    rank = latent.shape[2] // 2
    vmem = pl.BlockSpec(memory_space=pltpu.VMEM)
    return pl.pallas_call(
        attend_kernel,
        out_shape=jax.ShapeDtypeStruct((3, heads, rank), jnp.float32),
        in_specs=[pl.BlockSpec(memory_space=pltpu.SMEM), vmem, vmem, vmem],
        out_specs=vmem,
        name="attend",
    )(lengths, latent, up_key, queries)


def joined(first, second):
    largest = jnp.maximum(first[1], second[1])
    factor_a = jnp.exp(first[1] - largest)
    factor_b = jnp.exp(second[1] - largest)
    return jnp.stack(
        [
            first[0] * factor_a + second[0] * factor_b,
            largest,
            first[2] * factor_a + second[2] * factor_b,
        ]
    )


def finish_kernel(mine, theirs, up_value, out):
    heads = out.shape[0]
    head_dim = out.shape[1]
    per_group = up_value.shape[2] // head_dim
    per_kv = heads // per_group
    both = joined(mine, theirs)
    mean = both[0] / both[2]
    parts = jnp.concatenate([p.astype(jnp.float32) for p in split(mean, 3)], axis=0)
    wide = lax.dot_general(
        parts.astype(jnp.bfloat16),
        up_value[lax.axis_index("grp")],
        (((1,), (0,)), ((), ())),
        preferred_element_type=jnp.float32,
    )
    full = wide[2 * heads :] + wide[heads : 2 * heads] + wide[:heads]
    for k in range(per_group):
        rows = slice(k * per_kv, (k + 1) * per_kv)
        out[rows, :] = full[rows, k * head_dim : (k + 1) * head_dim]


def finish(mine, theirs, up_value, head_dim):
    vmem = pl.BlockSpec(memory_space=pltpu.VMEM)
    return pl.pallas_call(
        finish_kernel,
        out_shape=jax.ShapeDtypeStruct((mine.shape[1], head_dim), jnp.float32),
        in_specs=[vmem, vmem, vmem],
        out_specs=vmem,
        name="finish",
    )(mine, theirs, up_value)


def swap(x, axis, mask):
    return lax.ppermute(x, axis, [(i, i ^ mask) for i in range(lax.axis_size(axis))])


def body(latent, up_key, up_value, queries, lengths, block_dest):
    groups = up_key.shape[0]
    dests = latent.shape[1]
    batch, q_heads, head_dim = queries.shape
    heads = q_heads // groups
    outgoing = slotted(latent[0], block_dest)
    received = lax.all_to_all(outgoing, GRP_SEQ, split_axis=0, concat_axis=0, tiled=True)
    decode_latent = received.reshape(1, groups, dests // groups, *latent.shape[2:])

    partial = attend(latent[0], up_key, queries, lengths, heads)
    partial = joined(partial, swap(partial, "seq_2", 1))
    block = finish(partial, swap(partial, "seq_1", 1), up_value, head_dim)[None]
    own = {axis: lax.axis_index(axis) for axis in ("grp", "seq_0", "seq_1")}
    for axis, masks in (("seq_1", (3,)), ("seq_0", (1, 3)), ("grp", (1, 3))):
        for mask in masks:
            block = jnp.concatenate([block, swap(block, axis, mask)])
    g = jnp.arange(groups)[None, :]
    seq = jnp.arange(batch)[:, None]

    def place(wanted, here):
        high = (wanted >> 1) ^ (here >> 1)
        return 2 * high + ((wanted ^ here) & 1 ^ high)

    at = (
        place(g, own["grp"]) * 8
        + place(seq >> 1, own["seq_0"]) * 2
        + ((seq & 1) ^ (own["seq_1"] >> 1))
    )
    attended = block[at].reshape(batch, q_heads * head_dim)
    return (decode_latent, attended)


def solution(mesh):
    finer = Mesh(
        mesh.devices.reshape(mesh.shape["grp"], 4, 4, 2), ("grp", "seq_0", "seq_1", "seq_2")
    )
    in_specs = (P("grp", SEQ, None, None), P(), P(), P(), P(), P())
    out_specs = (P(GRP_SEQ, None, None, None, None), P())
    return jax.shard_map(body, mesh=finer, in_specs=in_specs, out_specs=out_specs, check_vma=False)
```

time: 82.5 us -> 134 us (1.62)
  Pallas kernels: 0 us -> 70.3 us
  blocking collectives: 46.3 us -> 0 us
  waiting for transfers between devices: 0.01 us -> 25.3 us
  starting transfers between devices: 11.7 us -> 28.6 us
  matrix products: 10.4 us -> 0 us
  local copies, waits for them, and re-layouts: 10.2 us -> 4.11 us
    pallas_call x0 -> x3, Pallas kernels: none -> 70.3 us  [the longest x1 65.3 us: slotted(): pl.pallas_call(slot_kernel, out_shape=jax.ShapeDtypeStruct(latent.shape,...]
    all_gather x4 -> x0, blocking collectives: 46.3 us -> none  [the longest x3 32.9 us: all_in_one(): both, at, found = (lax.all_gather(jnp.concatenate(lines), axis), 0, {})]
    ppermute x0 -> x7, waiting for transfers between devices: none -> 25.3 us  [swap(): lax.ppermute(x, axis, [(i, i ^ mask) for i in range(lax.axis_size(axis))])]
    ppermute x0 -> x7, starting transfers between devices: none -> 17.4 us  [swap(): lax.ppermute(x, axis, [(i, i ^ mask) for i in range(lax.axis_size(axis))])]
    dot_general x7 -> x0, matrix products: 10.4 us -> none  [the longest x1 3.68 us: partials(): jnp.einsum('gskjt,gstkd->gskjd', weights, values, precision=highest)]
    gather x1, local copies, waits for them, and re-layouts: 3.59 us -> 0.59 us  [body(): attended = block[at].reshape(batch, q_heads * head_dim)]
    concatenate x0 -> x3, other arithmetic: none -> 2.1 us  [body(): block = jnp.concatenate([block, swap(block, axis, mask)])]
    unnamed x13 -> x9, local copies, waits for them, and re-layouts: 4.61 us -> 2.67 us
  transfers between devices with their start and end apart: 1 -> 8, of which waited for: 0 -> 7; matrix products, arithmetic and copies ran while one was open for 17% -> 4% of each run, Pallas kernels for 0% -> 4%
where the time goes in v1:
time: 134 us; the launch traced here: 133 us
  Pallas kernels  70.3 us (52%)
  starting transfers between devices  28.6 us (21%)
  waiting for transfers between devices  25.3 us (19%)
  local copies, waits for them, and re-layouts  4.11 us (3%)
  other arithmetic  3.66 us (3%)
    pallas_call x1, Pallas kernels, slotted(): pl.pallas_call(slot_kernel, out_shape=jax.ShapeDtypeStruct(latent.shape,...  65.3 us
    ppermute x7, waiting for transfers between devices, swap(): lax.ppermute(x, axis, [(i, i ^ mask) for i in range(lax.axis_size(axis))])  25.3 us
    ppermute x7, starting transfers between devices, swap(): lax.ppermute(x, axis, [(i, i ^ mask) for i in range(lax.axis_size(axis))])  17.4 us
    all_to_all x1, starting transfers between devices, body(): lax.all_to_all(outgoing, GRP_SEQ, split_axis=0, concat_axis=0, tiled=True)  11.2 us
    pallas_call x1, Pallas kernels, attend(): pl.pallas_call(attend_kernel, out_shape=jax.ShapeDtypeStruct((3, heads, r...  3.21 us
  transfers between devices with their start and end apart: 8, of which 7 were waited for; matrix products, arithmetic and copies ran while one was open for 4% of the time, Pallas kernels for 4%

profile of v1, /device:TPU:0, one launch (start us, length us, event | category | flops | bytes accessed | tf_op | source)
XLA Modules:
  0.0 132.7 jit_solution(8252280878529342938)
XLA Ops:
  0.6 65.3 %slot.1 = bf16[128,32,256]{2,1,0:T(8,128)(2,1)} custom-call(s32[4096]{0:T(1024)} %dests.1, bf16[128,32,256]{2,1,0:T(8,128)(2,1)} %bitcast.7), custom_call_target="tpu_custom_call" | custom-call | tf_op jit(solution)/shard_map/slot/pallas_call | solution.py:31
  66.0 11.2 %all-to-all-start = ((bf16[128,32,256]{2,1,0:T(8,128)(2,1)}), bf16[128,32,256]{2,1,0:T(8,128)(2,1)S(1)}, u32[]{:S(2)}, u32[]{:S(2)}) async-start(bf16[128,32,256]{2,1,0:T(8,128)(2,1)} %slot.1), calls=%async_computation | async-start | bytes 4194304 | tf_op jit(solution)/shard_map/all_to_all | solution.py:173
  77.1 3.2 %attend.1 = f32[3,16,128]{2,1,0:T(8,128)} custom-call(s32[8]{0:T(128)} %lengths.1, bf16[128,32,256]{2,1,0:T(8,128)(2,1)} %bitcast.8, bf16[4,128,256]{2,1,0:T(8,128)(2,1)} %up_key.1, bf16[8,64,128]{2,1,0:T(8,128)(2,1)} %queries.1), custom_call_target="tpu_custom_call" | custom-call | tf_op jit(solution)/shard_map/attend/pallas_call | solution.py:110
  80.4 0.0 collective-permute-start
  80.4 1.4 %collective-permute-done = f32[3,16,128]{2,1,0:T(8,128)S(1)} collective-permute-done((f32[3,16,128]{2,1,0:T(8,128)}, f32[3,16,128]{2,1,0:T(8,128)S(1)}, u32[]{:S(2)}, u32[]{:S(2)}) %collective-permute-start) | collective-permute-done | bytes 24608 | tf_op jit(solution)/shard_map/ppermute | solution.py:164
  81.8 0.7 fusion.1
  82.5 0.7 fusion
  83.2 0.0 copy-start
  83.3 1.1 collective-permute-start.1
  84.3 13.9 %collective-permute-done.1.theirs = f32[3,16,128]{2,1,0:T(8,128)S(1)} collective-permute-done((f32[3,16,128]{2,1,0:T(8,128)S(1)}, f32[3,16,128]{2,1,0:T(8,128)S(1)}, u32[]{:S(2)}, u32[]{:S(2)}) %collective-permute-start.1) | collective-permute-done | bytes 24608 | tf_op jit(solution)/shard_map/ppermute | solution.py:164
  98.2 0.6 copy-done.1
  98.8 1.7 %finish.1 = f32[16,128]{1,0:T(8,128)} custom-call(f32[3,16,128]{2,1,0:T(8,128)} %copy-done, f32[3,16,128]{2,1,0:T(8,128)} %copy-done.1, bf16[4,128,256]{2,1,0:T(8,128)(2,1)} %up_value.1), custom_call_target="tpu_custom_call" | custom-call | tf_op jit(solution)/shard_map/finish/pallas_call | solution.py:154
  100.5 4.6 %collective-permute-start.2 = (f32[1,16,128]{2,1,0:T(8,128)}, f32[1,16,128]{2,1,0:T(8,128)S(1)}, u32[]{:S(2)}, u32[]{:S(2)}) collective-permute-start(f32[1,16,128]{2,1,0:T(8,128)} %bitcast.10), channel_id=1, source_target_pairs={{0,6},{2,4},{4,2},{6,0},{1,7},{3,5},{5,3},{7,1},{8,14},{10,12},{12... | collective-permute-start | bytes 24584 | tf_op jit(solution)/shard_map/ppermute | solution.py:164
  105.2 0.7 constant_dynamic-update-slice_fusion.4
  105.9 1.1 collective-permute-done.2
  107.0 0.7 pad_maximum_fusion.3
  107.7 3.3 %collective-permute-start.3 = (f32[2,16,128]{2,1,0:T(8,128)S(1)}, f32[2,16,128]{2,1,0:T(8,128)S(1)}, u32[]{:S(2)}, u32[]{:S(2)}) collective-permute-start(f32[2,16,128]{2,1,0:T(8,128)S(1)} %pad_maximum_fusion.3), channel_id=1, source_target_pairs={{0,8},{8,0},{16,24},{24,16},{1,9},{9,1},{17,25},{25,17},{2,10},{10... | collective-permute-start | bytes 49160 | tf_op jit(solution)/shard_map/ppermute | solution.py:164
  111.0 1.7 %collective-permute-done.3 = f32[2,16,128]{2,1,0:T(8,128)S(1)} collective-permute-done((f32[2,16,128]{2,1,0:T(8,128)S(1)}, f32[2,16,128]{2,1,0:T(8,128)S(1)}, u32[]{:S(2)}, u32[]{:S(2)}) %collective-permute-start.3) | collective-permute-done | bytes 16416 | tf_op jit(solution)/shard_map/ppermute | solution.py:164
  112.7 0.7 pad_maximum_fusion.1
  113.4 3.2 %collective-permute-start.4 = (f32[4,16,128]{2,1,0:T(8,128)S(1)}, f32[4,16,128]{2,1,0:T(8,128)S(1)}, u32[]{:S(2)}, u32[]{:S(2)}) collective-permute-start(f32[4,16,128]{2,1,0:T(8,128)S(1)} %pad_maximum_fusion.1), channel_id=1, source_target_pairs={{0,24},{8,16},{16,8},{24,0},{1,25},{9,17},{17,9},{25,1},{2,26},{10... | collective-permute-start | bytes 98312 | tf_op jit(solution)/shard_map/ppermute | solution.py:164
  116.6 1.9 %collective-permute-done.4 = f32[4,16,128]{2,1,0:T(8,128)S(1)} collective-permute-done((f32[4,16,128]{2,1,0:T(8,128)S(1)}, f32[4,16,128]{2,1,0:T(8,128)S(1)}, u32[]{:S(2)}, u32[]{:S(2)}) %collective-permute-start.4) | collective-permute-done | bytes 32800 | tf_op jit(solution)/shard_map/ppermute | solution.py:164
  118.5 0.7 pad_maximum_fusion
  119.2 1.7 %collective-permute-start.5 = (f32[8,16,128]{2,1,0:T(8,128)S(1)}, f32[8,16,128]{2,1,0:T(8,128)S(1)}, u32[]{:S(2)}, u32[]{:S(2)}) collective-permute-start(f32[8,16,128]{2,1,0:T(8,128)S(1)} %pad_maximum_fusion), channel_id=1, source_target_pairs={{0,32},{32,0},{64,96},{96,64},{1,33},{33,1},{65,97},{97,65},{2,34}... | collective-permute-start | bytes 196616 | tf_op jit(solution)/shard_map/ppermute | solution.py:164
  120.9 2.6 %collective-permute-done.5 = f32[8,16,128]{2,1,0:T(8,128)S(1)} collective-permute-done((f32[8,16,128]{2,1,0:T(8,128)S(1)}, f32[8,16,128]{2,1,0:T(8,128)S(1)}, u32[]{:S(2)}, u32[]{:S(2)}) %collective-permute-start.5) | collective-permute-done | bytes 65568 | tf_op jit(solution)/shard_map/ppermute | solution.py:164
  123.5 3.5 %collective-permute-start.6 = (f32[16,16,128]{2,1,0:T(8,128)S(1)}, f32[16,16,128]{2,1,0:T(8,128)S(1)}, u32[]{:S(2)}, u32[]{:S(2)}) collective-permute-start(f32[16,16,128]{2,1,0:T(8,128)S(1)} %get-tuple-element.4), channel_id=1, source_target_pairs={{0,96},{32,64},{64,32},{96,0},{1,97},{33,65},{65,33},{97,1},{2,98}... | collective-permute-start | bytes 393224 | tf_op jit(solution)/shard_map/ppermute | solution.py:164
  127.0 0.1 compare_select_fusion
  127.1 0.1 reshape.139
  127.2 2.8 %collective-permute-done.6 = f32[16,16,128]{2,1,0:T(8,128)S(1)} collective-permute-done((f32[16,16,128]{2,1,0:T(8,128)S(1)}, f32[16,16,128]{2,1,0:T(8,128)S(1)}, u32[]{:S(2)}, u32[]{:S(2)}) %collective-permute-start.6) | collective-permute-done | bytes 131104 | tf_op jit(solution)/shard_map/ppermute | solution.py:164
  130.0 0.6 gather_fusion
  130.6 0.8 reshape.136
  131.3 0.0 all-to-all-done
  131.4 1.3 copy.18
  (11 shorter events, 0.1 us)
Async XLA Ops:
  66.0 65.4 %all-to-all-start = ((bf16[128,32,256]{2,1,0:T(8,128)(2,1)}), bf16[128,32,256]{2,1,0:T(8,128)(2,1)S(1)}, u32[]{:S(2)}, u32[]{:S(2)}) async-start(bf16[128,32,256]{2,1,0:T(8,128)(2,1)} %slot.1), calls=%async_computation | async-start | bytes 4194304 | tf_op jit(solution)/shard_map/all_to_all | solution.py:173
  80.4 1.4 %collective-permute-start = (f32[3,16,128]{2,1,0:T(8,128)}, f32[3,16,128]{2,1,0:T(8,128)S(1)}, u32[]{:S(2)}, u32[]{:S(2)}) collective-permute-start(f32[3,16,128]{2,1,0:T(8,128)} %attend.1), channel_id=1, source_target_pairs={{0,1},{1,0},{2,3},{3,2},{4,5},{5,4},{6,7},{7,6},{8,9},{9,8},{10,11... | collective-permute-start | bytes 73736 | tf_op jit(solution)/shard_map/ppermute | solution.py:164
  83.2 15.0 %copy-start = (f32[3,16,128]{2,1,0:T(8,128)}, f32[3,16,128]{2,1,0:T(8,128)S(1)}, u32[]{:S(2)}) copy-start(f32[3,16,128]{2,1,0:T(8,128)S(1)} %pad_maximum_fusion.2.mine) | copy-start | bytes 73732
  83.3 15.0 %collective-permute-start.1 = (f32[3,16,128]{2,1,0:T(8,128)S(1)}, f32[3,16,128]{2,1,0:T(8,128)S(1)}, u32[]{:S(2)}, u32[]{:S(2)}) collective-permute-start(f32[3,16,128]{2,1,0:T(8,128)S(1)} %pad_maximum_fusion.2.mine), channel_id=1, source_target_pairs={{0,2},{2,0},{4,6},{6,4},{1,3},{3,1},{5,7},{7,5},{8,10},{10,8},{12,... | collective-permute-start | bytes 73736 | tf_op jit(solution)/shard_map/ppermute | solution.py:164
  98.2 0.6 copy-start.1
  100.5 6.4 %collective-permute-start.2 = (f32[1,16,128]{2,1,0:T(8,128)}, f32[1,16,128]{2,1,0:T(8,128)S(1)}, u32[]{:S(2)}, u32[]{:S(2)}) collective-permute-start(f32[1,16,128]{2,1,0:T(8,128)} %bitcast.10), channel_id=1, source_target_pairs={{0,6},{2,4},{4,2},{6,0},{1,7},{3,5},{5,3},{7,1},{8,14},{10,12},{12... | collective-permute-start | bytes 24584 | tf_op jit(solution)/shard_map/ppermute | solution.py:164
  107.7 5.0 %collective-permute-start.3 = (f32[2,16,128]{2,1,0:T(8,128)S(1)}, f32[2,16,128]{2,1,0:T(8,128)S(1)}, u32[]{:S(2)}, u32[]{:S(2)}) collective-permute-start(f32[2,16,128]{2,1,0:T(8,128)S(1)} %pad_maximum_fusion.3), channel_id=1, source_target_pairs={{0,8},{8,0},{16,24},{24,16},{1,9},{9,1},{17,25},{25,17},{2,10},{10... | collective-permute-start | bytes 49160 | tf_op jit(solution)/shard_map/ppermute | solution.py:164
  113.4 5.1 %collective-permute-start.4 = (f32[4,16,128]{2,1,0:T(8,128)S(1)}, f32[4,16,128]{2,1,0:T(8,128)S(1)}, u32[]{:S(2)}, u32[]{:S(2)}) collective-permute-start(f32[4,16,128]{2,1,0:T(8,128)S(1)} %pad_maximum_fusion.1), channel_id=1, source_target_pairs={{0,24},{8,16},{16,8},{24,0},{1,25},{9,17},{17,9},{25,1},{2,26},{10... | collective-permute-start | bytes 98312 | tf_op jit(solution)/shard_map/ppermute | solution.py:164
  119.2 4.3 %collective-permute-start.5 = (f32[8,16,128]{2,1,0:T(8,128)S(1)}, f32[8,16,128]{2,1,0:T(8,128)S(1)}, u32[]{:S(2)}, u32[]{:S(2)}) collective-permute-start(f32[8,16,128]{2,1,0:T(8,128)S(1)} %pad_maximum_fusion), channel_id=1, source_target_pairs={{0,32},{32,0},{64,96},{96,64},{1,33},{33,1},{65,97},{97,65},{2,34}... | collective-permute-start | bytes 196616 | tf_op jit(solution)/shard_map/ppermute | solution.py:164
  123.5 6.5 %collective-permute-start.6 = (f32[16,16,128]{2,1,0:T(8,128)S(1)}, f32[16,16,128]{2,1,0:T(8,128)S(1)}, u32[]{:S(2)}, u32[]{:S(2)}) collective-permute-start(f32[16,16,128]{2,1,0:T(8,128)S(1)} %get-tuple-element.4), channel_id=1, source_target_pairs={{0,96},{32,64},{64,32},{96,0},{1,97},{33,65},{65,33},{97,1},{2,98}... | collective-permute-start | bytes 393224 | tf_op jit(solution)/shard_map/ppermute | solution.py:164

commit v2 on v1

v2 whole, which is shorter than its diff:
```python
import jax
import jax.numpy as jnp
from jax import lax
from jax.experimental import pallas as pl
from jax.experimental.pallas import tpu as pltpu
from jax.sharding import Mesh
from jax.sharding import PartitionSpec as P

SEQ = ("seq_0", "seq_1", "seq_2")
GRP_SEQ = ("grp", "seq_0", "seq_1", "seq_2")
NEG = -1e30
VMEM = pl.BlockSpec(memory_space=pltpu.VMEM)
SMEM = pl.BlockSpec(memory_space=pltpu.SMEM)
PARAMS = pltpu.CompilerParams(vmem_limit_bytes=16 << 20)


def split(x, parts):
    pieces = []
    for _ in range(parts):
        piece = x.astype(jnp.bfloat16).astype(jnp.float32)
        pieces.append(piece)
        x = x - piece
    return jnp.concatenate(pieces, axis=0).astype(jnp.bfloat16)


def attend_kernel(lengths, latent, up_key, queries, out):
    blocks, block_len, width = latent.shape
    rank = width // 2
    tokens = blocks * block_len
    heads = out.shape[1]
    head_dim = queries.shape[2]
    per_group = up_key.shape[2] // head_dim
    per_kv = heads // per_group
    shard = lax.axis_index(SEQ)
    group = lax.axis_index("grp")
    quarter = lax.axis_size(SEQ) // queries.shape[0]
    seq = shard // quarter
    live_count = lengths[seq] - (shard % quarter) * tokens
    query = queries[seq, pl.ds(pl.multiple_of(group * heads, heads), heads), :]
    query = query.astype(jnp.float32)
    key_map = up_key[group]
    rows = [
        lax.dot_general(
            query[k * per_kv : (k + 1) * per_kv].astype(jnp.bfloat16),
            key_map[:, k * head_dim : (k + 1) * head_dim],
            (((1,), (1,)), ((), ())),
            preferred_element_type=jnp.float32,
        )
        for k in range(per_group)
    ]
    absorbed = jnp.concatenate(rows, axis=0) * (1.0 / float(head_dim) ** 0.5)
    lat = latent[...].reshape(tokens, width)
    raw = lax.dot_general(
        split(absorbed, 3),
        lat[:, :rank],
        (((1,), (1,)), ((), ())),
        preferred_element_type=jnp.float32,
    )
    scores = raw[2 * heads :] + raw[heads : 2 * heads] + raw[:heads]
    live = lax.broadcasted_iota(jnp.int32, (heads, tokens), 1) < live_count
    scores = jnp.where(live, scores, NEG)
    largest = jnp.max(scores, axis=1, keepdims=True)
    weights = jnp.where(live, jnp.exp(scores - largest), 0.0)
    total = jnp.sum(weights, axis=1, keepdims=True)
    summed = lax.dot_general(
        split(weights, 2),
        lat[:, rank:],
        (((1,), (0,)), ((), ())),
        preferred_element_type=jnp.float32,
    )
    out[0] = summed[:heads] + summed[heads:]
    out[1] = jnp.broadcast_to(largest, (heads, rank))
    out[2] = jnp.broadcast_to(total, (heads, rank))


def attend(latent, up_key, queries, lengths, heads):
    rank = latent.shape[2] // 2
    return pl.pallas_call(
        attend_kernel,
        out_shape=jax.ShapeDtypeStruct((3, heads, rank), jnp.float32),
        in_specs=[SMEM, VMEM, VMEM, VMEM],
        out_specs=VMEM,
        compiler_params=PARAMS,
        name="attend",
    )(lengths, latent, up_key, queries)


def joined(first, second):
    largest = jnp.maximum(first[1], second[1])
    factor_a = jnp.exp(first[1] - largest)
    factor_b = jnp.exp(second[1] - largest)
    accum = first[0] * factor_a + second[0] * factor_b
    return (accum, largest, first[2] * factor_a + second[2] * factor_b)


def merge_kernel(mine, theirs, out):
    kept = out.shape[1]
    rows = pl.ds(pl.multiple_of(lax.axis_index("seq_2") * kept, kept), kept)
    both = joined(
        [mine[i, rows, :] for i in range(3)], [theirs[i, rows, :] for i in range(3)]
    )
    for i in range(3):
        out[i] = both[i]


def merge(mine, theirs):
    return pl.pallas_call(
        merge_kernel,
        out_shape=jax.ShapeDtypeStruct((3, mine.shape[1] // 2, mine.shape[2]), jnp.float32),
        in_specs=[VMEM, VMEM],
        out_specs=VMEM,
        compiler_params=PARAMS,
        name="merge",
    )(mine, theirs)


def pack_kernel(table, latent, mine, theirs, up_value, out):
    blocks, block_len, width = latent.shape
    rank = width // 2
    head_dim = mine.shape[2]
    accum, _, total = joined([mine[i] for i in range(3)], [theirs[i] for i in range(3)])
    mean = accum / total
    half = mean.shape[0] // 2
    mean = jnp.where(lax.axis_index("seq_1") % 2 == 1, mean[half:], mean[:half])
    value_map = up_value[lax.axis_index("grp")]
    value_map = jnp.where(
        lax.axis_index("seq_2") == 1, value_map[:, head_dim:], value_map[:, :head_dim]
    )
    wide = lax.dot_general(
        split(mean, 3), value_map, (((1,), (0,)), ((), ())), preferred_element_type=jnp.float32
    )
    extra = split(wide[2 * half :] + wide[half : 2 * half] + wide[:half], 2)

    def place(b, carry):
        to = table[b]
        out[to, :block_len, :] = latent[b, :, :rank]
        out[to, block_len : 2 * block_len, :] = latent[b, :, rank:]
        out[b, 2 * block_len :, :] = extra
        return carry

    lax.fori_loop(0, blocks, place, 0, unroll=4)


def pack(table, latent, mine, theirs, up_value):
    blocks, block_len, width = latent.shape
    rows = 2 * block_len + mine.shape[1]
    return pl.pallas_call(
        pack_kernel,
        out_shape=jax.ShapeDtypeStruct((blocks, rows, width // 2), latent.dtype),
        in_specs=[SMEM, VMEM, VMEM, VMEM, VMEM],
        out_specs=VMEM,
        compiler_params=PARAMS,
        name="pack",
    )(table, latent, mine, theirs, up_value)


def unpack_kernel(received, decode, attended, sems):
    sources, rows, rank = received.shape
    _, _, _, block_len, _ = decode.shape
    groups = lax.axis_size("grp")
    shards = sources // groups
    copies = []
    for g in range(groups):
        for k in range(2):
            copies.append(
                pltpu.make_async_copy(
                    received.at[pl.ds(g * shards, shards), pl.ds(k * block_len, block_len), :],
                    decode.at[0, g, :, :, pl.ds(k * rank, rank)],
                    sems.at[g, k],
                )
            )
    for c in copies:
        c.start()
    half = (rows - 2 * block_len) // 2
    for s in range(sources):
        g, x, y, c = s // 32, s // 8 % 4, s // 2 % 4, s % 2
        seq = 2 * x + y // 2
        part = received[s, 2 * block_len :, :].astype(jnp.float32)
        part = part[half:] + part[:half]
        first = g * 16 + c * 8 + y % 2 * 4
        for j in range(half):
            attended[seq : seq + 1, (first + j) * rank : (first + j + 1) * rank] = part[j : j + 1]
    for c in copies:
        c.wait()


def unpack(received, groups, batch, heads, block_len):
    sources, _, rank = received.shape
    return pl.pallas_call(
        unpack_kernel,
        out_shape=(
            jax.ShapeDtypeStruct(
                (1, groups, sources // groups, block_len, 2 * rank), received.dtype
            ),
            jax.ShapeDtypeStruct((batch, heads * rank), jnp.float32),
        ),
        in_specs=[VMEM],
        out_specs=(pl.BlockSpec(memory_space=pl.ANY), VMEM),
        scratch_shapes=[pltpu.SemaphoreType.DMA((groups, 2))],
        compiler_params=PARAMS,
        name="unpack",
    )(received)


def swap(x, axis, mask):
    return lax.ppermute(x, axis, [(i, i ^ mask) for i in range(lax.axis_size(axis))])


def body(latent, up_key, up_value, queries, lengths, block_dest):
    groups = up_key.shape[0]
    dests = latent.shape[1]
    block_len = latent.shape[2]
    batch, q_heads, _ = queries.shape
    table = lax.dynamic_slice_in_dim(block_dest, lax.axis_index(SEQ) * dests, dests)
    part = attend(latent[0], up_key, queries, lengths, q_heads // groups)
    part = merge(part, swap(part, "seq_2", 1))
    outgoing = pack(table, latent[0], part, swap(part, "seq_1", 1), up_value)
    received = lax.all_to_all(outgoing, GRP_SEQ, split_axis=0, concat_axis=0, tiled=True)
    return unpack(received, groups, batch, q_heads, block_len)


def solution(mesh):
    finer = Mesh(
        mesh.devices.reshape(mesh.shape["grp"], 4, 4, 2), ("grp", "seq_0", "seq_1", "seq_2")
    )
    in_specs = (P("grp", SEQ, None, None), P(), P(), P(), P(), P())
    out_specs = (P(GRP_SEQ, None, None, None, None), P())
    return jax.shard_map(body, mesh=finer, in_specs=in_specs, out_specs=out_specs, check_vma=False)
```

time: 134 us -> 59 us (0.44)
  Pallas kernels: 70.3 us -> 4.74 us
  blocking collectives: 0 us -> 44.1 us
  starting transfers between devices: 28.6 us -> 1.87 us
  waiting for transfers between devices: 25.3 us -> 2.41 us
  other arithmetic: 3.66 us -> 0 us
    pallas_call x2 -> x3, Pallas kernels: 67.1 us -> 3.3 us  [the longest x1 2.07 us: unpack(): pl.pallas_call(unpack_kernel, out_shape=(jax.ShapeDtypeStruct((1, groups,...]
    all_to_all x0 -> x1, blocking collectives: none -> 44.1 us  [body(): lax.all_to_all(outgoing, GRP_SEQ, split_axis=0, concat_axis=0, tiled=True)]
    ppermute x7 -> x2, waiting for transfers between devices: 25.3 us -> 2.41 us  [swap(): lax.ppermute(x, axis, [(i, i ^ mask) for i in range(lax.axis_size(axis))])]
    ppermute x7 -> x2, starting transfers between devices: 17.4 us -> 1.87 us  [swap(): lax.ppermute(x, axis, [(i, i ^ mask) for i in range(lax.axis_size(axis))])]
    all_to_all x1 -> x0, starting transfers between devices: 11.2 us -> none  [body(): lax.all_to_all(outgoing, GRP_SEQ, split_axis=0, concat_axis=0, tiled=True)]
    concatenate x3 -> x0, other arithmetic: 2.1 us -> none  [body(): block = jnp.concatenate([block, swap(block, axis, mask)])]
    pallas_call x1, Pallas kernels: 3.21 us -> 1.44 us  [attend(): pl.pallas_call(attend_kernel, out_shape=jax.ShapeDtypeStruct((3, heads, r...]
    add x2 -> x0, other arithmetic: 1.45 us -> none  [the longest x1 0.73 us: joined(): first[2] * factor_a + second[2] * factor_b]
  transfers between devices with their start and end apart: 8 -> 2, of which waited for: 7 -> 2; matrix products, arithmetic and copies ran while one was open for 4% -> 1% of each run, Pallas kernels for 4% -> 0%
where the time goes in v2:
time: 59 us; the launch traced here: 58.7 us
  blocking collectives  44.1 us (75%)
  local copies, waits for them, and re-layouts  4.86 us (8%)
  Pallas kernels  4.74 us (8%)
  waiting for transfers between devices  2.41 us (4%)
  starting transfers between devices  1.87 us (3%)
  between operations  0.67 us (1%)
    all_to_all x1, blocking collectives, body(): lax.all_to_all(outgoing, GRP_SEQ, split_axis=0, concat_axis=0, tiled=True)  44.1 us
    unnamed x12, local copies, waits for them, and re-layouts  4.1 us
    ppermute x2, waiting for transfers between devices, swap(): lax.ppermute(x, axis, [(i, i ^ mask) for i in range(lax.axis_size(axis))])  2.41 us
    pallas_call x1, Pallas kernels, unpack(): pl.pallas_call(unpack_kernel, out_shape=(jax.ShapeDtypeStruct((1, groups,...  2.07 us
    ppermute x2, starting transfers between devices, swap(): lax.ppermute(x, axis, [(i, i ^ mask) for i in range(lax.axis_size(axis))])  1.87 us
    pallas_call x1, Pallas kernels, attend(): pl.pallas_call(attend_kernel, out_shape=jax.ShapeDtypeStruct((3, heads, r...  1.44 us
    pallas_call x1, Pallas kernels, pack(): pl.pallas_call(pack_kernel, out_shape=jax.ShapeDtypeStruct((blocks, rows,...  1.21 us
  transfers between devices with their start and end apart: 2, of which 2 were waited for; matrix products, arithmetic and copies ran while one was open for 1% of the time, Pallas kernels for 0%

profile of v2, /device:TPU:0, one launch (start us, length us, event | category | flops | bytes accessed | tf_op | source)
XLA Modules:
  0.0 58.7 jit_solution(666841038470789098)
XLA Ops:
  0.6 0.0 copy-start
  0.6 1.6 %copy-done = bf16[1,128,32,256]{3,2,1,0:T(8,128)(2,1)S(1)} copy-done((bf16[1,128,32,256]{3,2,1,0:T(8,128)(2,1)S(1)}, bf16[1,128,32,256]{3,2,1,0:T(8,128)(2,1)}, u32[]{:S(2)}) %copy-start) | copy-done | bytes 2097176
  2.2 0.0 copy-start.3
  2.2 0.9 %copy-done.3 = bf16[4,128,256]{2,1,0:T(8,128)(2,1)S(1)} copy-done((bf16[4,128,256]{2,1,0:T(8,128)(2,1)S(1)}, bf16[4,128,256]{2,1,0:T(8,128)(2,1)}, u32[]{:S(2)}) %copy-start.3) | copy-done | bytes 262168
  3.2 0.0 copy-start.4
  3.2 0.9 %copy-done.4 = bf16[8,64,128]{2,1,0:T(8,128)(2,1)S(1)} copy-done((bf16[8,64,128]{2,1,0:T(8,128)(2,1)S(1)}, bf16[8,64,128]{2,1,0:T(8,128)(2,1)}, u32[]{:S(2)}) %copy-start.4) | copy-done | bytes 131096
  4.1 0.0 copy-start.5
  4.1 0.7 %copy-done.5 = s32[8]{0:T(128)S(1)} copy-done((s32[8]{0:T(128)S(1)}, s32[8]{0:T(128)}, u32[]{:S(2)}) %copy-start.5) | copy-done | bytes 56
  4.7 0.0 copy-start.1
  4.7 0.0 copy-start.2
  4.7 1.4 %attend.1.mine = f32[3,16,128]{2,1,0:T(8,128)S(1)} custom-call(s32[8]{0:T(128)S(1)} %copy-done.5, bf16[128,32,256]{2,1,0:T(8,128)(2,1)S(1)} %bitcast.1, bf16[4,128,256]{2,1,0:T(8,128)(2,1)S(1)} %copy-done.3, bf16[8,64,128]{2,1,0:T(8,128)(2,1)S(1)} %copy-done.4), custom_call_target="tpu_custom_call" | custom-call | tf_op jit(solution)/shard_map/attend/pallas_call | solution.py:78
  6.2 0.1 collective-permute-start
  6.3 1.2 %collective-permute-done.theirs = f32[3,16,128]{2,1,0:T(8,128)S(1)} collective-permute-done((f32[3,16,128]{2,1,0:T(8,128)S(1)}, f32[3,16,128]{2,1,0:T(8,128)S(1)}, u32[]{:S(2)}, u32[]{:S(2)}) %collective-permute-start) | collective-permute-done | bytes 24608 | tf_op jit(solution)/shard_map/ppermute | solution.py:206
  7.5 1.8 %collective-permute-start.1 = (f32[3,8,128]{2,1,0:T(8,128)S(1)}, f32[3,8,128]{2,1,0:T(8,128)S(1)}, u32[]{:S(2)}, u32[]{:S(2)}) collective-permute-start(f32[3,8,128]{2,1,0:T(8,128)S(1)} %merge.1.mine), channel_id=1, source_target_pairs={{0,2},{2,0},{4,6},{6,4},{1,3},{3,1},{5,7},{7,5},{8,10},{10,8},{12,... | collective-permute-start | bytes 36872 | tf_op jit(solution)/shard_map/ppermute | solution.py:206
  9.3 0.8 %dynamic_slice.3.table = s32[128]{0:T(128)S(1)} dynamic-slice(s32[4096]{0:T(1024)} %param.11, s32[]{:T(128)S(6)} %select_n.3), dynamic_slice_sizes={128} | dynamic-slice | bytes 1028 | tf_op jit(solution)/shard_map/dynamic_slice | solution.py:214
  10.0 1.2 %collective-permute-done.1.theirs = f32[3,8,128]{2,1,0:T(8,128)S(1)} collective-permute-done((f32[3,8,128]{2,1,0:T(8,128)S(1)}, f32[3,8,128]{2,1,0:T(8,128)S(1)}, u32[]{:S(2)}, u32[]{:S(2)}) %collective-permute-start.1) | collective-permute-done | bytes 12320 | tf_op jit(solution)/shard_map/ppermute | solution.py:206
  11.3 0.0 copy-done.1
  11.3 0.0 copy-done.2
  11.3 1.2 %pack.1 = bf16[128,72,128]{2,1,0:T(8,128)(2,1)S(1)} custom-call(s32[128]{0:T(128)S(1)} %dynamic_slice.3.table, bf16[128,32,256]{2,1,0:T(8,128)(2,1)S(1)} %bitcast.2, f32[3,8,128]{2,1,0:T(8,128)S(1)} %merge.1.mine, f32[3,8,128]{2,1,0:T(8,128)S(1)} %collective-permute-done.1.theirs, bf16[4,128,256]{2,1,0:T(8,128)(2,1)S(1)} %copy-done.2), custom_call_target="tpu_custom_call" | custom-call | tf_op jit(solution)/shard_map/pack/pallas_call | solution.py:147
  12.5 44.1 %all_to_all.5.received = bf16[128,72,128]{2,1,0:T(8,128)(2,1)S(1)} all-to-all(bf16[128,72,128]{2,1,0:T(8,128)(2,1)S(1)} %pack.1), channel_id=1, replica_groups=mesh['grp'=4,'seq_0'=4,'seq_1'=4,'seq_2'=2] {'grp','seq_0','seq_1','seq_2'}, dimensions={0} | all-to-all | bytes 4718592 | tf_op jit(solution)/shard_map/all_to_all | solution.py:218
  56.6 2.1 %unpack.1 = (bf16[1,4,32,32,256]{4,3,2,1,0:T(8,128)(2,1)}, f32[8,8192]{1,0:T(8,128)}) custom-call(bf16[128,72,128]{2,1,0:T(8,128)(2,1)S(1)} %all_to_all.5.received), custom_call_target="tpu_custom_call" | custom-call | tf_op jit(solution)/shard_map/unpack/pallas_call | solution.py:189
  (1 shorter events, 0.0 us)
Async XLA Ops:
  0.6 1.6 %copy-start = (bf16[1,128,32,256]{3,2,1,0:T(8,128)(2,1)S(1)}, bf16[1,128,32,256]{3,2,1,0:T(8,128)(2,1)}, u32[]{:S(2)}) copy-start(bf16[1,128,32,256]{3,2,1,0:T(8,128)(2,1)} %param.6) | copy-start | bytes 6291460
  2.2 0.9 %copy-start.3 = (bf16[4,128,256]{2,1,0:T(8,128)(2,1)S(1)}, bf16[4,128,256]{2,1,0:T(8,128)(2,1)}, u32[]{:S(2)}) copy-start(bf16[4,128,256]{2,1,0:T(8,128)(2,1)} %up_key.1) | copy-start | bytes 786436
  3.2 0.9 %copy-start.4 = (bf16[8,64,128]{2,1,0:T(8,128)(2,1)S(1)}, bf16[8,64,128]{2,1,0:T(8,128)(2,1)}, u32[]{:S(2)}) copy-start(bf16[8,64,128]{2,1,0:T(8,128)(2,1)} %queries.1) | copy-start | bytes 393220
  4.1 0.7 %copy-start.5 = (s32[8]{0:T(128)S(1)}, s32[8]{0:T(128)}, u32[]{:S(2)}) copy-start(s32[8]{0:T(128)} %lengths.1) | copy-start | bytes 100
  4.7 6.5 %copy-start.1 = (bf16[1,128,32,256]{3,2,1,0:T(8,128)(2,1)S(1)}, bf16[1,128,32,256]{3,2,1,0:T(8,128)(2,1)}, u32[]{:S(2)}) copy-start(bf16[1,128,32,256]{3,2,1,0:T(8,128)(2,1)} %param.6) | copy-start | bytes 6291460
  4.7 6.5 %copy-start.2 = (bf16[4,128,256]{2,1,0:T(8,128)(2,1)S(1)}, bf16[4,128,256]{2,1,0:T(8,128)(2,1)}, u32[]{:S(2)}) copy-start(bf16[4,128,256]{2,1,0:T(8,128)(2,1)} %up_value.1) | copy-start | bytes 786436
  6.2 1.3 %collective-permute-start = (f32[3,16,128]{2,1,0:T(8,128)S(1)}, f32[3,16,128]{2,1,0:T(8,128)S(1)}, u32[]{:S(2)}, u32[]{:S(2)}) collective-permute-start(f32[3,16,128]{2,1,0:T(8,128)S(1)} %attend.1.mine), channel_id=1, source_target_pairs={{0,1},{1,0},{2,3},{3,2},{4,5},{5,4},{6,7},{7,6},{8,9},{9,8},{10,11... | collective-permute-start | bytes 73736 | tf_op jit(solution)/shard_map/ppermute | solution.py:206
  7.5 3.8 %collective-permute-start.1 = (f32[3,8,128]{2,1,0:T(8,128)S(1)}, f32[3,8,128]{2,1,0:T(8,128)S(1)}, u32[]{:S(2)}, u32[]{:S(2)}) collective-permute-start(f32[3,8,128]{2,1,0:T(8,128)S(1)} %merge.1.mine), channel_id=1, source_target_pairs={{0,2},{2,0},{4,6},{6,4},{1,3},{3,1},{5,7},{7,5},{8,10},{10,8},{12,... | collective-permute-start | bytes 36872 | tf_op jit(solution)/shard_map/ppermute | solution.py:206

commit v3 on v2

v3 whole, which is shorter than its diff:
```python
import jax
import jax.numpy as jnp
from jax import lax
from jax.experimental import pallas as pl
from jax.experimental.pallas import tpu as pltpu
from jax.sharding import Mesh
from jax.sharding import PartitionSpec as P

SEQ = ("seq_0", "seq_1", "seq_2")
GRP_SEQ = ("grp", "seq_0", "seq_1", "seq_2")
NEG = -1e30
VMEM = pl.BlockSpec(memory_space=pltpu.VMEM)
HBM = pl.BlockSpec(memory_space=pltpu.HBM)
PARAMS = pltpu.CompilerParams(vmem_limit_bytes=16 << 20)


def split(x, parts):
    pieces = []
    for _ in range(parts):
        piece = x.astype(jnp.bfloat16).astype(jnp.float32)
        pieces.append(piece)
        x = x - piece
    return jnp.concatenate(pieces, axis=0).astype(jnp.bfloat16)


def attend_kernel(
    ends, dests, latent, up_key, queries, out, outgoing, lat, key_map, query, table, lengths, sems
):
    chunks, per_chunk, block_len, width = lat.shape
    rank = width // 2
    tokens = per_chunk * block_len
    heads, head_dim = query.shape
    per_group = key_map.shape[1] // head_dim
    per_kv = heads // per_group
    shard = lax.axis_index(SEQ)
    group = lax.axis_index("grp")
    quarter = lax.axis_size(SEQ) // queries.shape[0]
    seq = shard // quarter
    count = chunks * per_chunk
    small = [
        pltpu.make_async_copy(
            queries.at[seq, pl.ds(pl.multiple_of(group * heads, heads), heads)], query, sems.at[0]
        ),
        pltpu.make_async_copy(up_key.at[group], key_map, sems.at[1]),
        pltpu.make_async_copy(
            dests.at[pl.ds(pl.multiple_of(shard * count, count), count)], table, sems.at[2]
        ),
        pltpu.make_async_copy(ends, lengths, sems.at[3]),
    ]
    large = [
        pltpu.make_async_copy(latent.at[pl.ds(i * per_chunk, per_chunk)], lat.at[i], sems.at[4 + i])
        for i in range(chunks)
    ]
    for copy in small + large:
        copy.start()
    for copy in small:
        copy.wait()
    live_count = lengths[seq] - (shard % quarter) * (chunks * tokens)
    heads_f = query[...].astype(jnp.float32)
    rows = [
        lax.dot_general(
            heads_f[k * per_kv : (k + 1) * per_kv].astype(jnp.bfloat16),
            key_map[:, k * head_dim : (k + 1) * head_dim],
            (((1,), (1,)), ((), ())),
            preferred_element_type=jnp.float32,
        )
        for k in range(per_group)
    ]
    absorbed = split(jnp.concatenate(rows, axis=0) * (1.0 / float(head_dim) ** 0.5), 3)
    found = []
    for i in range(chunks):
        large[i].wait()
        both = lat[i].reshape(tokens, width)
        raw = lax.dot_general(
            absorbed,
            both[:, :rank],
            (((1,), (1,)), ((), ())),
            preferred_element_type=jnp.float32,
        )
        scores = raw[2 * heads :] + raw[heads : 2 * heads] + raw[:heads]
        position = lax.broadcasted_iota(jnp.int32, (heads, tokens), 1) + i * tokens
        live = position < live_count
        scores = jnp.where(live, scores, NEG)
        largest = jnp.max(scores, axis=1, keepdims=True)
        weights = jnp.where(live, jnp.exp(scores - largest), 0.0)
        total = jnp.sum(weights, axis=1, keepdims=True)
        summed = lax.dot_general(
            split(weights, 2),
            both[:, rank:],
            (((1,), (0,)), ((), ())),
            preferred_element_type=jnp.float32,
        )
        found.append((summed[:heads] + summed[heads:], largest, total))
        for j in range(per_chunk):
            to = table[i * per_chunk + j]
            outgoing[to, :block_len, :] = lat[i, j, :, :rank]
            outgoing[to, block_len : 2 * block_len, :] = lat[i, j, :, rank:]
    largest = found[0][1]
    for _, other, _ in found[1:]:
        largest = jnp.maximum(largest, other)
    factors = [jnp.exp(f[1] - largest) for f in found]
    out[0] = sum(f[0] * k for f, k in zip(found, factors))
    out[1] = jnp.broadcast_to(largest, (heads, rank))
    out[2] = jnp.broadcast_to(sum(f[2] * k for f, k in zip(found, factors)), (heads, rank))


def attend(latent, up_key, queries, lengths, block_dest, chunks, extra):
    count, block_len, width = latent.shape
    groups = up_key.shape[0]
    _, q_heads, head_dim = queries.shape
    heads = q_heads // groups
    rank = width // 2
    return pl.pallas_call(
        attend_kernel,
        out_shape=(
            jax.ShapeDtypeStruct((3, heads, rank), jnp.float32),
            jax.ShapeDtypeStruct((count, 2 * block_len + extra, rank), latent.dtype),
        ),
        in_specs=[HBM] * 5,
        out_specs=(VMEM, VMEM),
        scratch_shapes=[
            pltpu.VMEM((chunks, count // chunks, block_len, width), latent.dtype),
            pltpu.VMEM(up_key.shape[1:], up_key.dtype),
            pltpu.VMEM((heads, head_dim), queries.dtype),
            pltpu.SMEM((count,), jnp.int32),
            pltpu.SMEM(lengths.shape, jnp.int32),
            pltpu.SemaphoreType.DMA((4 + chunks,)),
        ],
        compiler_params=PARAMS,
        name="attend",
    )(lengths, block_dest, latent, up_key, queries)


def joined(first, second):
    largest = jnp.maximum(first[1], second[1])
    factor_a = jnp.exp(first[1] - largest)
    factor_b = jnp.exp(second[1] - largest)
    accum = first[0] * factor_a + second[0] * factor_b
    return (accum, largest, first[2] * factor_a + second[2] * factor_b)


def merge_kernel(mine, theirs, out):
    kept = out.shape[1]
    rows = pl.ds(pl.multiple_of(lax.axis_index("seq_2") * kept, kept), kept)
    both = joined(
        [mine[i, rows, :] for i in range(3)], [theirs[i, rows, :] for i in range(3)]
    )
    for i in range(3):
        out[i] = both[i]


def merge(mine, theirs):
    return pl.pallas_call(
        merge_kernel,
        out_shape=jax.ShapeDtypeStruct((3, mine.shape[1] // 2, mine.shape[2]), jnp.float32),
        in_specs=[VMEM, VMEM],
        out_specs=VMEM,
        compiler_params=PARAMS,
        name="merge",
    )(mine, theirs)


def pack_kernel(mine, theirs, up_value, _, out):
    head_dim = mine.shape[2]
    accum, _, total = joined([mine[i] for i in range(3)], [theirs[i] for i in range(3)])
    mean = accum / total
    half = mean.shape[0] // 2
    mean = jnp.where(lax.axis_index("seq_1") % 2 == 1, mean[half:], mean[:half])
    value_map = up_value[lax.axis_index("grp")]
    value_map = jnp.where(
        lax.axis_index("seq_2") == 1, value_map[:, head_dim:], value_map[:, :head_dim]
    )
    wide = lax.dot_general(
        split(mean, 3), value_map, (((1,), (0,)), ((), ())), preferred_element_type=jnp.float32
    )
    extra = split(wide[2 * half :] + wide[half : 2 * half] + wide[:half], 2)
    rows = out.shape[1] - extra.shape[0]
    for b in range(out.shape[0]):
        out[b, rows:, :] = extra


def pack(mine, theirs, up_value, outgoing):
    return pl.pallas_call(
        pack_kernel,
        out_shape=jax.ShapeDtypeStruct(outgoing.shape, outgoing.dtype),
        in_specs=[VMEM] * 4,
        out_specs=VMEM,
        input_output_aliases={3: 0},
        compiler_params=PARAMS,
        name="pack",
    )(mine, theirs, up_value, outgoing)


def unpack_kernel(received, decode, attended, rows_out, sems, row_sems):
    sources, rows, rank = received.shape
    _, groups, shards, block_len, _ = decode.shape
    copies = []
    for g in range(groups):
        for k in range(2):
            copies.append(
                pltpu.make_async_copy(
                    received.at[pl.ds(g * shards, shards), pl.ds(k * block_len, block_len), :],
                    decode.at[0, g, :, :, pl.ds(k * rank, rank)],
                    sems.at[g, k],
                )
            )
    for c in copies:
        c.start()
    half = (rows - 2 * block_len) // 2
    span = rows_out.shape[1] // groups
    for g in range(groups):
        for s in range(shards):
            x, y, c = s // 8, s // 2 % 4, s % 2
            seq = 2 * x + y // 2
            part = received[g * shards + s, 2 * block_len :, :].astype(jnp.float32)
            part = part[half:] + part[:half]
            first = g * 16 + c * 8 + y % 2 * 4
            for j in range(half):
                at = (first + j) * rank
                rows_out[seq : seq + 1, at : at + rank] = part[j : j + 1]
        columns = pl.ds(g * span, span)
        copy = pltpu.make_async_copy(
            rows_out.at[:, columns], attended.at[:, columns], row_sems.at[g]
        )
        copy.start()
        copies.append(copy)
    for c in copies:
        c.wait()


def unpack(received, groups, batch, heads, block_len):
    sources, _, rank = received.shape
    return pl.pallas_call(
        unpack_kernel,
        out_shape=(
            jax.ShapeDtypeStruct(
                (1, groups, sources // groups, block_len, 2 * rank), received.dtype
            ),
            jax.ShapeDtypeStruct((batch, heads * rank), jnp.float32),
        ),
        in_specs=[VMEM],
        out_specs=(HBM, HBM),
        scratch_shapes=[
            pltpu.VMEM((batch, heads * rank), jnp.float32),
            pltpu.SemaphoreType.DMA((groups, 2)),
            pltpu.SemaphoreType.DMA((groups,)),
        ],
        compiler_params=PARAMS,
        name="unpack",
    )(received)


def swap(x, axis, mask):
    return lax.ppermute(x, axis, [(i, i ^ mask) for i in range(lax.axis_size(axis))])


def body(latent, up_key, up_value, queries, lengths, block_dest):
    groups = up_key.shape[0]
    block_len = latent.shape[2]
    batch, q_heads, _ = queries.shape
    part, outgoing = attend(latent[0], up_key, queries, lengths, block_dest, 4, 8)
    part = merge(part, swap(part, "seq_2", 1))
    outgoing = pack(part, swap(part, "seq_1", 1), up_value, outgoing)
    received = lax.all_to_all(outgoing, GRP_SEQ, split_axis=0, concat_axis=0, tiled=True)
    return unpack(received, groups, batch, q_heads, block_len)


def solution(mesh):
    finer = Mesh(
        mesh.devices.reshape(mesh.shape["grp"], 4, 4, 2), ("grp", "seq_0", "seq_1", "seq_2")
    )
    in_specs = (P("grp", SEQ, None, None), P(), P(), P(), P(), P())
    out_specs = (P(GRP_SEQ, None, None, None, None), P())
    return jax.shard_map(body, mesh=finer, in_specs=in_specs, out_specs=out_specs, check_vma=False)
```

time: 59 us -> 59.7 us (1.012)
  waiting for transfers between devices: 2.41 us -> 3.19 us
    ppermute x2, waiting for transfers between devices: 2.41 us -> 3.19 us  [swap(): lax.ppermute(x, axis, [(i, i ^ mask) for i in range(lax.axis_size(axis))])]
    dynamic_slice x1 -> x0, local copies, waits for them, and re-layouts: 0.76 us -> none  [body(): lax.dynamic_slice_in_dim(block_dest, lax.axis_index(SEQ) * dests, dests)]
    unnamed x12, local copies, waits for them, and re-layouts: 4.1 us -> 4.81 us
  transfers between devices with their start and end apart: 2 -> 2, of which waited for: 2 -> 2; matrix products, arithmetic and copies ran while one was open for 1% -> 0% of each run, Pallas kernels for 0% -> 0%
where the time goes in v3:
time: 59.7 us; the launch traced here: 59.3 us
  blocking collectives  44.1 us (74%)
  local copies, waits for them, and re-layouts  4.81 us (8%)
  Pallas kernels  4.68 us (8%)
  waiting for transfers between devices  3.19 us (5%)
  starting transfers between devices  1.85 us (3%)
  between operations  0.67 us (1%)
    all_to_all x1, blocking collectives, body(): lax.all_to_all(outgoing, GRP_SEQ, split_axis=0, concat_axis=0, tiled=True)  44.1 us
    unnamed x12, local copies, waits for them, and re-layouts  4.81 us
    ppermute x2, waiting for transfers between devices, swap(): lax.ppermute(x, axis, [(i, i ^ mask) for i in range(lax.axis_size(axis))])  3.19 us
    pallas_call x1, Pallas kernels, attend(): pl.pallas_call(attend_kernel, out_shape=(jax.ShapeDtypeStruct((3, heads,...  3 us
    ppermute x2, starting transfers between devices, swap(): lax.ppermute(x, axis, [(i, i ^ mask) for i in range(lax.axis_size(axis))])  1.85 us
    pallas_call x1, Pallas kernels, unpack(): pl.pallas_call(unpack_kernel, out_shape=(jax.ShapeDtypeStruct((1, groups,...  1.48 us
  transfers between devices with their start and end apart: 2, of which 2 were waited for; matrix products, arithmetic and copies ran while one was open for 0% of the time, Pallas kernels for 0%

profile of v3, /device:TPU:0, one launch (start us, length us, event | category | flops | bytes accessed | tf_op | source)
XLA Modules:
  0.0 59.3 jit_solution(1366139905020913163)
XLA Ops:
  0.6 0.0 copy-start
  0.6 1.6 %copy-done = bf16[1,128,32,256]{3,2,1,0:T(8,128)(2,1)S(1)} copy-done((bf16[1,128,32,256]{3,2,1,0:T(8,128)(2,1)S(1)}, bf16[1,128,32,256]{3,2,1,0:T(8,128)(2,1)}, u32[]{:S(2)}) %copy-start) | copy-done | bytes 2097176
  2.2 0.0 copy-start.2
  2.2 0.9 %copy-done.2 = bf16[4,128,256]{2,1,0:T(8,128)(2,1)S(1)} copy-done((bf16[4,128,256]{2,1,0:T(8,128)(2,1)S(1)}, bf16[4,128,256]{2,1,0:T(8,128)(2,1)}, u32[]{:S(2)}) %copy-start.2) | copy-done | bytes 262168
  3.2 0.0 copy-start.3
  3.2 0.9 %copy-done.3 = bf16[8,64,128]{2,1,0:T(8,128)(2,1)S(1)} copy-done((bf16[8,64,128]{2,1,0:T(8,128)(2,1)S(1)}, bf16[8,64,128]{2,1,0:T(8,128)(2,1)}, u32[]{:S(2)}) %copy-start.3) | copy-done | bytes 131096
  4.1 0.0 copy-start.4
  4.1 0.7 %copy-done.4 = s32[4096]{0:T(1024)S(1)} copy-done((s32[4096]{0:T(1024)S(1)}, s32[4096]{0:T(1024)}, u32[]{:S(2)}) %copy-start.4) | copy-done | bytes 16408
  4.8 0.0 copy-start.5
  4.8 0.7 %copy-done.5 = s32[8]{0:T(128)S(1)} copy-done((s32[8]{0:T(128)S(1)}, s32[8]{0:T(128)}, u32[]{:S(2)}) %copy-start.5) | copy-done | bytes 56
  5.5 0.0 copy-start.1
  5.5 3.0 %attend.1 = (f32[3,16,128]{2,1,0:T(8,128)S(1)}, bf16[128,72,128]{2,1,0:T(8,128)(2,1)S(1)}) custom-call(s32[8]{0:T(128)S(1)} %copy-done.5, s32[4096]{0:T(1024)S(1)} %copy-done.4, bf16[128,32,256]{2,1,0:T(8,128)(2,1)S(1)} %bitcast.1, bf16[4,128,256]{2,1,0:T(8,128)(2,1)S(1)} %copy-done.2, bf16[8,64,128]{2,1,0:T(8,128)(2,1)S(1)} %copy-done.3), custom_call_target="tpu_custom_call" | custom-call | tf_op jit(solution)/shard_map/attend/pallas_call | solution.py:113
  8.5 0.1 collective-permute-start
  8.6 1.2 %collective-permute-done.theirs = f32[3,16,128]{2,1,0:T(8,128)S(1)} collective-permute-done((f32[3,16,128]{2,1,0:T(8,128)S(1)}, f32[3,16,128]{2,1,0:T(8,128)S(1)}, u32[]{:S(2)}, u32[]{:S(2)}) %collective-permute-start) | collective-permute-done | bytes 24608 | tf_op jit(solution)/shard_map/ppermute | solution.py:254
  9.8 1.8 %collective-permute-start.1 = (f32[3,8,128]{2,1,0:T(8,128)S(1)}, f32[3,8,128]{2,1,0:T(8,128)S(1)}, u32[]{:S(2)}, u32[]{:S(2)}) collective-permute-start(f32[3,8,128]{2,1,0:T(8,128)S(1)} %merge.1.mine), channel_id=1, source_target_pairs={{0,2},{2,0},{4,6},{6,4},{1,3},{3,1},{5,7},{7,5},{8,10},{10,8},{12,... | collective-permute-start | bytes 36872 | tf_op jit(solution)/shard_map/ppermute | solution.py:254
  11.5 2.0 %collective-permute-done.1.theirs = f32[3,8,128]{2,1,0:T(8,128)S(1)} collective-permute-done((f32[3,8,128]{2,1,0:T(8,128)S(1)}, f32[3,8,128]{2,1,0:T(8,128)S(1)}, u32[]{:S(2)}, u32[]{:S(2)}) %collective-permute-start.1) | collective-permute-done | bytes 12320 | tf_op jit(solution)/shard_map/ppermute | solution.py:254
  13.5 0.0 copy-done.1
  13.5 0.2 pack.1
  13.7 44.1 %all_to_all.5.received = bf16[128,72,128]{2,1,0:T(8,128)(2,1)S(1)} all-to-all(bf16[128,72,128]{2,1,0:T(8,128)(2,1)S(1)} %pack.1), channel_id=1, replica_groups=mesh['grp'=4,'seq_0'=4,'seq_1'=4,'seq_2'=2] {'grp','seq_0','seq_1','seq_2'}, dimensions={0} | all-to-all | bytes 4718592 | tf_op jit(solution)/shard_map/all_to_all | solution.py:264
  57.8 1.5 %unpack.1 = (bf16[1,4,32,32,256]{4,3,2,1,0:T(8,128)(2,1)}, f32[8,8192]{1,0:T(8,128)}) custom-call(bf16[128,72,128]{2,1,0:T(8,128)(2,1)S(1)} %all_to_all.5.received), custom_call_target="tpu_custom_call" | custom-call | tf_op jit(solution)/shard_map/unpack/pallas_call | solution.py:233
  (1 shorter events, 0.0 us)
Async XLA Ops:
  0.6 1.6 %copy-start = (bf16[1,128,32,256]{3,2,1,0:T(8,128)(2,1)S(1)}, bf16[1,128,32,256]{3,2,1,0:T(8,128)(2,1)}, u32[]{:S(2)}) copy-start(bf16[1,128,32,256]{3,2,1,0:T(8,128)(2,1)} %param.6) | copy-start | bytes 6291460
  2.2 0.9 %copy-start.2 = (bf16[4,128,256]{2,1,0:T(8,128)(2,1)S(1)}, bf16[4,128,256]{2,1,0:T(8,128)(2,1)}, u32[]{:S(2)}) copy-start(bf16[4,128,256]{2,1,0:T(8,128)(2,1)} %up_key.1) | copy-start | bytes 786436
  3.2 0.9 %copy-start.3 = (bf16[8,64,128]{2,1,0:T(8,128)(2,1)S(1)}, bf16[8,64,128]{2,1,0:T(8,128)(2,1)}, u32[]{:S(2)}) copy-start(bf16[8,64,128]{2,1,0:T(8,128)(2,1)} %queries.1) | copy-start | bytes 393220
  4.1 0.7 %copy-start.4 = (s32[4096]{0:T(1024)S(1)}, s32[4096]{0:T(1024)}, u32[]{:S(2)}) copy-start(s32[4096]{0:T(1024)} %dests.1) | copy-start | bytes 49156
  4.8 0.7 %copy-start.5 = (s32[8]{0:T(128)S(1)}, s32[8]{0:T(128)}, u32[]{:S(2)}) copy-start(s32[8]{0:T(128)} %ends.1) | copy-start | bytes 100
  5.5 8.1 %copy-start.1 = (bf16[4,128,256]{2,1,0:T(8,128)(2,1)S(1)}, bf16[4,128,256]{2,1,0:T(8,128)(2,1)}, u32[]{:S(2)}) copy-start(bf16[4,128,256]{2,1,0:T(8,128)(2,1)} %up_value.1) | copy-start | bytes 786436
  8.5 1.3 %collective-permute-start = (f32[3,16,128]{2,1,0:T(8,128)S(1)}, f32[3,16,128]{2,1,0:T(8,128)S(1)}, u32[]{:S(2)}, u32[]{:S(2)}) collective-permute-start(f32[3,16,128]{2,1,0:T(8,128)S(1)} %get-tuple-element.4.mine), channel_id=1, source_target_pairs={{0,1},{1,0},{2,3},{3,2},{4,5},{5,4},{6,7},{7,6},{8,9},{9,8},{10,11... | collective-permute-start | bytes 73736 | tf_op jit(solution)/shard_map/ppermute | solution.py:254
  9.8 3.8 %collective-permute-start.1 = (f32[3,8,128]{2,1,0:T(8,128)S(1)}, f32[3,8,128]{2,1,0:T(8,128)S(1)}, u32[]{:S(2)}, u32[]{:S(2)}) collective-permute-start(f32[3,8,128]{2,1,0:T(8,128)S(1)} %merge.1.mine), channel_id=1, source_target_pairs={{0,2},{2,0},{4,6},{6,4},{1,3},{3,1},{5,7},{7,5},{8,10},{10,8},{12,... | collective-permute-start | bytes 36872 | tf_op jit(solution)/shard_map/ppermute | solution.py:254

commit v4 on v3

--- a/solution.py
+++ b/solution.py
@@ -128,7 +128,10 @@
         ],
         compiler_params=PARAMS,
         name="attend",
-    )(lengths, block_dest, latent, up_key, queries)
+    )(*[
+        pltpu.with_memory_space_constraint(x, pltpu.HBM)
+        for x in (lengths, block_dest, latent, up_key, queries)
+    ])
 
 
 def joined(first, second):

time: 59.7 us -> 55.1 us (0.923)
  local copies, waits for them, and re-layouts: 4.81 us -> 0.01 us
    unnamed x12 -> x2, local copies, waits for them, and re-layouts: 4.81 us -> 0.01 us
where the time goes in v4:
time: 55.1 us; the launch traced here: 54.9 us
  blocking collectives  44.1 us (80%)
  Pallas kernels  5.06 us (9%)
  waiting for transfers between devices  3.19 us (6%)
  starting transfers between devices  1.85 us (3%)
  between operations  0.67 us (1%)
    all_to_all x1, blocking collectives, body(): lax.all_to_all(outgoing, GRP_SEQ, split_axis=0, concat_axis=0, tiled=True)  44.1 us
    pallas_call x1, Pallas kernels, attend(): pl.pallas_call(attend_kernel, out_shape=(jax.ShapeDtypeStruct((3, heads,...  3.39 us
    ppermute x2, waiting for transfers between devices, swap(): lax.ppermute(x, axis, [(i, i ^ mask) for i in range(lax.axis_size(axis))])  3.19 us
    ppermute x2, starting transfers between devices, swap(): lax.ppermute(x, axis, [(i, i ^ mask) for i in range(lax.axis_size(axis))])  1.85 us
    pallas_call x1, Pallas kernels, unpack(): pl.pallas_call(unpack_kernel, out_shape=(jax.ShapeDtypeStruct((1, groups,...  1.48 us
  transfers between devices with their start and end apart: 2, of which 2 were waited for; matrix products, arithmetic and copies ran while one was open for 0% of the time, Pallas kernels for 0%

profile of v4, /device:TPU:0, one launch (start us, length us, event | category | flops | bytes accessed | tf_op | source)
XLA Modules:
  0.0 54.9 jit_solution(10145324963263204357)
XLA Ops:
  0.6 0.0 copy-start
  0.6 3.4 %attend.1 = (f32[3,16,128]{2,1,0:T(8,128)S(1)}, bf16[128,72,128]{2,1,0:T(8,128)(2,1)S(1)}) custom-call(s32[8]{0:T(128)} %ends.1, s32[4096]{0:T(1024)} %dests.1, bf16[128,32,256]{2,1,0:T(8,128)(2,1)} %bitcast.1, bf16[4,128,256]{2,1,0:T(8,128)(2,1)} %up_key.1, bf16[8,64,128]{2,1,0:T(8,128)(2,1)} %queries.1), custom_call_target="tpu_custom_call" | custom-call | tf_op jit(solution)/shard_map/attend/pallas_call | solution.py:113
  4.0 0.1 collective-permute-start
  4.1 1.2 %collective-permute-done.theirs = f32[3,16,128]{2,1,0:T(8,128)S(1)} collective-permute-done((f32[3,16,128]{2,1,0:T(8,128)S(1)}, f32[3,16,128]{2,1,0:T(8,128)S(1)}, u32[]{:S(2)}, u32[]{:S(2)}) %collective-permute-start) | collective-permute-done | bytes 24608 | tf_op jit(solution)/shard_map/ppermute | solution.py:257
  5.3 1.8 %collective-permute-start.1 = (f32[3,8,128]{2,1,0:T(8,128)S(1)}, f32[3,8,128]{2,1,0:T(8,128)S(1)}, u32[]{:S(2)}, u32[]{:S(2)}) collective-permute-start(f32[3,8,128]{2,1,0:T(8,128)S(1)} %merge.1.mine), channel_id=1, source_target_pairs={{0,2},{2,0},{4,6},{6,4},{1,3},{3,1},{5,7},{7,5},{8,10},{10,8},{12,... | collective-permute-start | bytes 36872 | tf_op jit(solution)/shard_map/ppermute | solution.py:257
  7.1 2.0 %collective-permute-done.1.theirs = f32[3,8,128]{2,1,0:T(8,128)S(1)} collective-permute-done((f32[3,8,128]{2,1,0:T(8,128)S(1)}, f32[3,8,128]{2,1,0:T(8,128)S(1)}, u32[]{:S(2)}, u32[]{:S(2)}) %collective-permute-start.1) | collective-permute-done | bytes 12320 | tf_op jit(solution)/shard_map/ppermute | solution.py:257
  9.1 0.0 copy-done
  9.1 0.2 pack.1
  9.3 44.1 %all_to_all.5.received = bf16[128,72,128]{2,1,0:T(8,128)(2,1)S(1)} all-to-all(bf16[128,72,128]{2,1,0:T(8,128)(2,1)S(1)} %pack.1), channel_id=1, replica_groups=mesh['grp'=4,'seq_0'=4,'seq_1'=4,'seq_2'=2] {'grp','seq_0','seq_1','seq_2'}, dimensions={0} | all-to-all | bytes 4718592 | tf_op jit(solution)/shard_map/all_to_all | solution.py:267
  53.4 1.5 %unpack.1 = (bf16[1,4,32,32,256]{4,3,2,1,0:T(8,128)(2,1)}, f32[8,8192]{1,0:T(8,128)}) custom-call(bf16[128,72,128]{2,1,0:T(8,128)(2,1)S(1)} %all_to_all.5.received), custom_call_target="tpu_custom_call" | custom-call | tf_op jit(solution)/shard_map/unpack/pallas_call | solution.py:236
  (1 shorter events, 0.0 us)
Async XLA Ops:
  0.6 8.5 %copy-start = (bf16[4,128,256]{2,1,0:T(8,128)(2,1)S(1)}, bf16[4,128,256]{2,1,0:T(8,128)(2,1)}, u32[]{:S(2)}) copy-start(bf16[4,128,256]{2,1,0:T(8,128)(2,1)} %up_value.1) | copy-start | bytes 786436
  4.0 1.3 %collective-permute-start = (f32[3,16,128]{2,1,0:T(8,128)S(1)}, f32[3,16,128]{2,1,0:T(8,128)S(1)}, u32[]{:S(2)}, u32[]{:S(2)}) collective-permute-start(f32[3,16,128]{2,1,0:T(8,128)S(1)} %get-tuple-element.4.mine), channel_id=1, source_target_pairs={{0,1},{1,0},{2,3},{3,2},{4,5},{5,4},{6,7},{7,6},{8,9},{9,8},{10,11... | collective-permute-start | bytes 73736 | tf_op jit(solution)/shard_map/ppermute | solution.py:257
  5.3 3.8 %collective-permute-start.1 = (f32[3,8,128]{2,1,0:T(8,128)S(1)}, f32[3,8,128]{2,1,0:T(8,128)S(1)}, u32[]{:S(2)}, u32[]{:S(2)}) collective-permute-start(f32[3,8,128]{2,1,0:T(8,128)S(1)} %merge.1.mine), channel_id=1, source_target_pairs={{0,2},{2,0},{4,6},{6,4},{1,3},{3,1},{5,7},{7,5},{8,10},{10,8},{12,... | collective-permute-start | bytes 36872 | tf_op jit(solution)/shard_map/ppermute | solution.py:257

commit v5 on v3

--- a/solution.py
+++ b/solution.py
@@ -24,11 +24,10 @@
 
 
 def attend_kernel(
-    ends, dests, latent, up_key, queries, out, outgoing, lat, key_map, query, table, lengths, sems
+    ends, latent, up_key, queries, out, key, value, key_map, query, lengths, sems
 ):
-    chunks, per_chunk, block_len, width = lat.shape
-    rank = width // 2
-    tokens = per_chunk * block_len
+    count, block_len, rank = key.shape
+    tokens = count * block_len
     heads, head_dim = query.shape
     per_group = key_map.shape[1] // head_dim
     per_kv = heads // per_group
@@ -36,26 +35,19 @@
     group = lax.axis_index("grp")
     quarter = lax.axis_size(SEQ) // queries.shape[0]
     seq = shard // quarter
-    count = chunks * per_chunk
-    small = [
-        pltpu.make_async_copy(
-            queries.at[seq, pl.ds(pl.multiple_of(group * heads, heads), heads)], query, sems.at[0]
-        ),
+    first = pl.multiple_of(group * heads, heads)
+    copies = [
+        pltpu.make_async_copy(queries.at[seq, pl.ds(first, heads)], query, sems.at[0]),
         pltpu.make_async_copy(up_key.at[group], key_map, sems.at[1]),
-        pltpu.make_async_copy(
-            dests.at[pl.ds(pl.multiple_of(shard * count, count), count)], table, sems.at[2]
-        ),
-        pltpu.make_async_copy(ends, lengths, sems.at[3]),
+        pltpu.make_async_copy(ends, lengths, sems.at[2]),
+        pltpu.make_async_copy(latent.at[:, :, pl.ds(0, rank)], key, sems.at[3]),
+        pltpu.make_async_copy(latent.at[:, :, pl.ds(rank, rank)], value, sems.at[4]),
     ]
-    large = [
-        pltpu.make_async_copy(latent.at[pl.ds(i * per_chunk, per_chunk)], lat.at[i], sems.at[4 + i])
-        for i in range(chunks)
-    ]
-    for copy in small + large:
+    for copy in copies:
         copy.start()
-    for copy in small:
+    for copy in copies[:3]:
         copy.wait()
-    live_count = lengths[seq] - (shard % quarter) * (chunks * tokens)
+    live_count = lengths[seq] - (shard % quarter) * tokens
     heads_f = query[...].astype(jnp.float32)
     rows = [
         lax.dot_general(
@@ -67,68 +59,83 @@
         for k in range(per_group)
     ]
     absorbed = split(jnp.concatenate(rows, axis=0) * (1.0 / float(head_dim) ** 0.5), 3)
-    found = []
-    for i in range(chunks):
-        large[i].wait()
-        both = lat[i].reshape(tokens, width)
-        raw = lax.dot_general(
-            absorbed,
-            both[:, :rank],
-            (((1,), (1,)), ((), ())),
-            preferred_element_type=jnp.float32,
-        )
-        scores = raw[2 * heads :] + raw[heads : 2 * heads] + raw[:heads]
-        position = lax.broadcasted_iota(jnp.int32, (heads, tokens), 1) + i * tokens
-        live = position < live_count
-        scores = jnp.where(live, scores, NEG)
-        largest = jnp.max(scores, axis=1, keepdims=True)
-        weights = jnp.where(live, jnp.exp(scores - largest), 0.0)
-        total = jnp.sum(weights, axis=1, keepdims=True)
-        summed = lax.dot_general(
-            split(weights, 2),
-            both[:, rank:],
-            (((1,), (0,)), ((), ())),
-            preferred_element_type=jnp.float32,
-        )
-        found.append((summed[:heads] + summed[heads:], largest, total))
-        for j in range(per_chunk):
-            to = table[i * per_chunk + j]
-            outgoing[to, :block_len, :] = lat[i, j, :, :rank]
-            outgoing[to, block_len : 2 * block_len, :] = lat[i, j, :, rank:]
-    largest = found[0][1]
-    for _, other, _ in found[1:]:
-        largest = jnp.maximum(largest, other)
-    factors = [jnp.exp(f[1] - largest) for f in found]
-    out[0] = sum(f[0] * k for f, k in zip(found, factors))
+    copies[3].wait()
+    raw = lax.dot_general(
+        absorbed,
+        key[...].reshape(tokens, rank),
+        (((1,), (1,)), ((), ())),
+        preferred_element_type=jnp.float32,
+    )
+    scores = raw[2 * heads :] + raw[heads : 2 * heads] + raw[:heads]
+    live = lax.broadcasted_iota(jnp.int32, (heads, tokens), 1) < live_count
+    scores = jnp.where(live, scores, NEG)
+    largest = jnp.max(scores, axis=1, keepdims=True)
+    weights = jnp.where(live, jnp.exp(scores - largest), 0.0)
+    total = jnp.sum(weights, axis=1, keepdims=True)
+    halves = split(weights, 2)
+    copies[4].wait()
+    summed = lax.dot_general(
+        halves,
+        value[...].reshape(tokens, rank),
+        (((1,), (0,)), ((), ())),
+        preferred_element_type=jnp.float32,
+    )
+    out[0] = summed[:heads] + summed[heads:]
     out[1] = jnp.broadcast_to(largest, (heads, rank))
-    out[2] = jnp.broadcast_to(sum(f[2] * k for f, k in zip(found, factors)), (heads, rank))
-
-
-def attend(latent, up_key, queries, lengths, block_dest, chunks, extra):
+    out[2] = jnp.broadcast_to(total, (heads, rank))
+
+
+def attend(latent, up_key, queries, lengths):
     count, block_len, width = latent.shape
-    groups = up_key.shape[0]
-    _, q_heads, head_dim = queries.shape
-    heads = q_heads // groups
+    heads = queries.shape[1] // up_key.shape[0]
     rank = width // 2
     return pl.pallas_call(
         attend_kernel,
         out_shape=(
             jax.ShapeDtypeStruct((3, heads, rank), jnp.float32),
-            jax.ShapeDtypeStruct((count, 2 * block_len + extra, rank), latent.dtype),
+            jax.ShapeDtypeStruct((count, block_len, rank), latent.dtype),
+            jax.ShapeDtypeStruct((count, block_len, rank), latent.dtype),
         ),
-        in_specs=[HBM] * 5,
-        out_specs=(VMEM, VMEM),
+        in_specs=[HBM] * 4,
+        out_specs=(VMEM,) * 3,
         scratch_shapes=[
-            pltpu.VMEM((chunks, count // chunks, block_len, width), latent.dtype),
             pltpu.VMEM(up_key.shape[1:], up_key.dtype),
-            pltpu.VMEM((heads, head_dim), queries.dtype),
-            pltpu.SMEM((count,), jnp.int32),
+            pltpu.VMEM((heads, queries.shape[2]), queries.dtype),
             pltpu.SMEM(lengths.shape, jnp.int32),
-            pltpu.SemaphoreType.DMA((4 + chunks,)),
+            pltpu.SemaphoreType.DMA((5,)),
         ],
         compiler_params=PARAMS,
         name="attend",
-    )(lengths, block_dest, latent, up_key, queries)
+    )(*[in_hbm(x) for x in (lengths, latent, up_key, queries)])
+
+
+def in_hbm(x):
+    return pltpu.with_memory_space_constraint(x, pltpu.HBM)
+
+
+def slot_kernel(dests, key, value, after, outgoing, table, sem):
+    count, block_len, _ = key.shape
+    first = pl.multiple_of(lax.axis_index(SEQ) * count, count)
+    copy = pltpu.make_async_copy(dests.at[pl.ds(first, count)], table, sem)
+    copy.start()
+    copy.wait()
+    for b in range(count):
+        to = table[b]
+        outgoing[to, :block_len, :] = key[b]
+        outgoing[to, block_len : 2 * block_len, :] = value[b]
+
+
+def slot(block_dest, key, value, after, extra):
+    count, block_len, rank = key.shape
+    return pl.pallas_call(
+        slot_kernel,
+        out_shape=jax.ShapeDtypeStruct((count, 2 * block_len + extra, rank), key.dtype),
+        in_specs=[HBM, VMEM, VMEM, VMEM],
+        out_specs=VMEM,
+        scratch_shapes=[pltpu.SMEM((count,), jnp.int32), pltpu.SemaphoreType.DMA],
+        compiler_params=PARAMS,
+        name="slot",
+    )(in_hbm(block_dest), key, value, after)
 
 
 def joined(first, second):
@@ -258,8 +265,9 @@
     groups = up_key.shape[0]
     block_len = latent.shape[2]
     batch, q_heads, _ = queries.shape
-    part, outgoing = attend(latent[0], up_key, queries, lengths, block_dest, 4, 8)
+    part, key, value = attend(latent[0], up_key, queries, lengths)
     part = merge(part, swap(part, "seq_2", 1))
+    outgoing = slot(block_dest, key, value, part, 8)
     outgoing = pack(part, swap(part, "seq_1", 1), up_value, outgoing)
     received = lax.all_to_all(outgoing, GRP_SEQ, split_axis=0, concat_axis=0, tiled=True)
     return unpack(received, groups, batch, q_heads, block_len)

time: 59.7 us -> 54.1 us (0.906)
  local copies, waits for them, and re-layouts: 4.81 us -> 0.01 us
  waiting for transfers between devices: 3.19 us -> 2.24 us
    unnamed x12 -> x2, local copies, waits for them, and re-layouts: 4.81 us -> 0.01 us
    ppermute x2, waiting for transfers between devices: 3.19 us -> 2.24 us  [swap(): lax.ppermute(x, axis, [(i, i ^ mask) for i in range(lax.axis_size(axis))])]
    pallas_call x0 -> x1, Pallas kernels: none -> 0.94 us  [slot(): pl.pallas_call(slot_kernel, out_shape=jax.ShapeDtypeStruct((count, 2 * bl...]
    pallas_call x1, Pallas kernels: 3 us -> 2.31 us  [attend(): pl.pallas_call(attend_kernel, out_shape=(jax.ShapeDtypeStruct((3, heads,...]
  transfers between devices with their start and end apart: 2 -> 2, of which waited for: 2 -> 2; matrix products, arithmetic and copies ran while one was open for 0% -> 0% of each run, Pallas kernels for 0% -> 2%
where the time goes in v5:
time: 54.1 us; the launch traced here: 53.8 us
  blocking collectives  44.1 us (82%)
  Pallas kernels  4.92 us (9%)
  waiting for transfers between devices  2.24 us (4%)
  starting transfers between devices  1.85 us (3%)
  between operations  0.67 us (1%)
    all_to_all x1, blocking collectives, body(): lax.all_to_all(outgoing, GRP_SEQ, split_axis=0, concat_axis=0, tiled=True)  44.1 us
    pallas_call x1, Pallas kernels, attend(): pl.pallas_call(attend_kernel, out_shape=(jax.ShapeDtypeStruct((3, heads,...  2.31 us
    ppermute x2, waiting for transfers between devices, swap(): lax.ppermute(x, axis, [(i, i ^ mask) for i in range(lax.axis_size(axis))])  2.24 us
    ppermute x2, starting transfers between devices, swap(): lax.ppermute(x, axis, [(i, i ^ mask) for i in range(lax.axis_size(axis))])  1.85 us
    pallas_call x1, Pallas kernels, unpack(): pl.pallas_call(unpack_kernel, out_shape=(jax.ShapeDtypeStruct((1, groups,...  1.48 us
  transfers between devices with their start and end apart: 2, of which 2 were waited for; matrix products, arithmetic and copies ran while one was open for 0% of the time, Pallas kernels for 2%

profile of v5, /device:TPU:0, one launch (start us, length us, event | category | flops | bytes accessed | tf_op | source)
XLA Modules:
  0.0 53.8 jit_solution(7128622912601986458)
XLA Ops:
  0.6 2.3 %attend.1 = (f32[3,16,128]{2,1,0:T(8,128)S(1)}, bf16[128,32,128]{2,1,0:T(8,128)(2,1)S(1)}, bf16[128,32,128]{2,1,0:T(8,128)(2,1)S(1)}) custom-call(s32[8]{0:T(128)} %ends.1, bf16[128,32,256]{2,1,0:T(8,128)(2,1)} %bitcast.1, bf16[4,128,256]{2,1,0:T(8,128)(2,1)} %up_key.1, bf16[8,64,128]{2,1,0:T(8,128)(2,1)} %queries.1), custom_call_target="tpu_custom_call" | custom-call | tf_op jit(solution)/shard_map/attend/pallas_call | solution.py:92
  2.9 0.0 copy-start
  3.0 0.1 collective-permute-start
  3.0 1.2 %collective-permute-done.theirs = f32[3,16,128]{2,1,0:T(8,128)S(1)} collective-permute-done((f32[3,16,128]{2,1,0:T(8,128)S(1)}, f32[3,16,128]{2,1,0:T(8,128)S(1)}, u32[]{:S(2)}, u32[]{:S(2)}) %collective-permute-start) | collective-permute-done | bytes 24608 | tf_op jit(solution)/shard_map/ppermute | solution.py:261
  4.2 1.8 %collective-permute-start.1 = (f32[3,8,128]{2,1,0:T(8,128)S(1)}, f32[3,8,128]{2,1,0:T(8,128)S(1)}, u32[]{:S(2)}, u32[]{:S(2)}) collective-permute-start(f32[3,8,128]{2,1,0:T(8,128)S(1)} %merge.1.after.mine), channel_id=1, source_target_pairs={{0,2},{2,0},{4,6},{6,4},{1,3},{3,1},{5,7},{7,5},{8,10},{10,8},{12,... | collective-permute-start | bytes 36872 | tf_op jit(solution)/shard_map/ppermute | solution.py:261
  6.0 0.9 %slot.1._ = bf16[128,72,128]{2,1,0:T(8,128)(2,1)S(1)} custom-call(s32[4096]{0:T(1024)} %dests.1, bf16[128,32,128]{2,1,0:T(8,128)(2,1)S(1)} %get-tuple-element.6.key, bf16[128,32,128]{2,1,0:T(8,128)(2,1)S(1)} %get-tuple-element.7.value, f32[3,8,128]{2,1,0:T(8,128)S(1)} %merge.1.after.mine), custom_call_target="tpu_custom_call" | custom-call | tf_op jit(solution)/shard_map/slot/pallas_call | solution.py:130
  7.0 1.1 %collective-permute-done.1.theirs = f32[3,8,128]{2,1,0:T(8,128)S(1)} collective-permute-done((f32[3,8,128]{2,1,0:T(8,128)S(1)}, f32[3,8,128]{2,1,0:T(8,128)S(1)}, u32[]{:S(2)}, u32[]{:S(2)}) %collective-permute-start.1) | collective-permute-done | bytes 12320 | tf_op jit(solution)/shard_map/ppermute | solution.py:261
  8.0 0.0 copy-done
  8.0 0.2 pack.1
  8.2 44.1 %all_to_all.5.received = bf16[128,72,128]{2,1,0:T(8,128)(2,1)S(1)} all-to-all(bf16[128,72,128]{2,1,0:T(8,128)(2,1)S(1)} %pack.1), channel_id=1, replica_groups=mesh['grp'=4,'seq_0'=4,'seq_1'=4,'seq_2'=2] {'grp','seq_0','seq_1','seq_2'}, dimensions={0} | all-to-all | bytes 4718592 | tf_op jit(solution)/shard_map/all_to_all | solution.py:272
  52.3 1.5 %unpack.1 = (bf16[1,4,32,32,256]{4,3,2,1,0:T(8,128)(2,1)}, f32[8,8192]{1,0:T(8,128)}) custom-call(bf16[128,72,128]{2,1,0:T(8,128)(2,1)S(1)} %all_to_all.5.received), custom_call_target="tpu_custom_call" | custom-call | tf_op jit(solution)/shard_map/unpack/pallas_call | solution.py:240
  (1 shorter events, 0.0 us)
Async XLA Ops:
  2.9 5.1 %copy-start = (bf16[4,128,256]{2,1,0:T(8,128)(2,1)S(1)}, bf16[4,128,256]{2,1,0:T(8,128)(2,1)}, u32[]{:S(2)}) copy-start(bf16[4,128,256]{2,1,0:T(8,128)(2,1)} %up_value.1) | copy-start | bytes 786436
  3.0 1.3 %collective-permute-start = (f32[3,16,128]{2,1,0:T(8,128)S(1)}, f32[3,16,128]{2,1,0:T(8,128)S(1)}, u32[]{:S(2)}, u32[]{:S(2)}) collective-permute-start(f32[3,16,128]{2,1,0:T(8,128)S(1)} %get-tuple-element.5.mine), channel_id=1, source_target_pairs={{0,1},{1,0},{2,3},{3,2},{4,5},{5,4},{6,7},{7,6},{8,9},{9,8},{10,11... | collective-permute-start | bytes 73736 | tf_op jit(solution)/shard_map/ppermute | solution.py:261
  4.2 3.8 %collective-permute-start.1 = (f32[3,8,128]{2,1,0:T(8,128)S(1)}, f32[3,8,128]{2,1,0:T(8,128)S(1)}, u32[]{:S(2)}, u32[]{:S(2)}) collective-permute-start(f32[3,8,128]{2,1,0:T(8,128)S(1)} %merge.1.after.mine), channel_id=1, source_target_pairs={{0,2},{2,0},{4,6},{6,4},{1,3},{3,1},{5,7},{7,5},{8,10},{10,8},{12,... | collective-permute-start | bytes 36872 | tf_op jit(solution)/shard_map/ppermute | solution.py:261

commit v6 on v3

--- a/solution.py
+++ b/solution.py
@@ -23,12 +23,12 @@
     return jnp.concatenate(pieces, axis=0).astype(jnp.bfloat16)
 
 
-def attend_kernel(
-    ends, dests, latent, up_key, queries, out, outgoing, lat, key_map, query, table, lengths, sems
-):
-    chunks, per_chunk, block_len, width = lat.shape
+def attend_kernel(ends, latent, up_key, queries, out, lat, key_map, query, lengths, sems):
+    count, block_len, width = lat.shape
+    chunks = sems.shape[0] - 3
+    blocks = count // chunks
+    tokens = blocks * block_len
     rank = width // 2
-    tokens = per_chunk * block_len
     heads, head_dim = query.shape
     per_group = key_map.shape[1] // head_dim
     per_kv = heads // per_group
@@ -36,26 +36,22 @@
     group = lax.axis_index("grp")
     quarter = lax.axis_size(SEQ) // queries.shape[0]
     seq = shard // quarter
-    count = chunks * per_chunk
+    first = pl.multiple_of(group * heads, heads)
     small = [
-        pltpu.make_async_copy(
-            queries.at[seq, pl.ds(pl.multiple_of(group * heads, heads), heads)], query, sems.at[0]
-        ),
+        pltpu.make_async_copy(queries.at[seq, pl.ds(first, heads)], query, sems.at[0]),
         pltpu.make_async_copy(up_key.at[group], key_map, sems.at[1]),
-        pltpu.make_async_copy(
-            dests.at[pl.ds(pl.multiple_of(shard * count, count), count)], table, sems.at[2]
-        ),
-        pltpu.make_async_copy(ends, lengths, sems.at[3]),
+        pltpu.make_async_copy(ends, lengths, sems.at[2]),
     ]
+    parts = [pl.ds(i * blocks, blocks) for i in range(chunks)]
     large = [
-        pltpu.make_async_copy(latent.at[pl.ds(i * per_chunk, per_chunk)], lat.at[i], sems.at[4 + i])
-        for i in range(chunks)
+        pltpu.make_async_copy(latent.at[part], lat.at[part], sems.at[3 + i])
+        for i, part in enumerate(parts)
     ]
     for copy in small + large:
         copy.start()
     for copy in small:
         copy.wait()
-    live_count = lengths[seq] - (shard % quarter) * (chunks * tokens)
+    live_count = lengths[seq] - (shard % quarter) * (count * block_len)
     heads_f = query[...].astype(jnp.float32)
     rows = [
         lax.dot_general(
@@ -67,68 +63,100 @@
         for k in range(per_group)
     ]
     absorbed = split(jnp.concatenate(rows, axis=0) * (1.0 / float(head_dim) ** 0.5), 3)
-    found = []
-    for i in range(chunks):
-        large[i].wait()
-        both = lat[i].reshape(tokens, width)
+
+    def scored(i):
         raw = lax.dot_general(
             absorbed,
-            both[:, :rank],
+            lat[parts[i], :, :rank].reshape(tokens, rank),
             (((1,), (1,)), ((), ())),
             preferred_element_type=jnp.float32,
         )
         scores = raw[2 * heads :] + raw[heads : 2 * heads] + raw[:heads]
         position = lax.broadcasted_iota(jnp.int32, (heads, tokens), 1) + i * tokens
         live = position < live_count
-        scores = jnp.where(live, scores, NEG)
+        return (jnp.where(live, scores, NEG), live)
+
+    def weighed(scores, live):
         largest = jnp.max(scores, axis=1, keepdims=True)
         weights = jnp.where(live, jnp.exp(scores - largest), 0.0)
-        total = jnp.sum(weights, axis=1, keepdims=True)
-        summed = lax.dot_general(
-            split(weights, 2),
-            both[:, rank:],
+        return (split(weights, 2), largest, jnp.sum(weights, axis=1, keepdims=True))
+
+    def summed(i, halves, largest, total):
+        both = lax.dot_general(
+            halves,
+            lat[parts[i], :, rank:].reshape(tokens, rank),
             (((1,), (0,)), ((), ())),
             preferred_element_type=jnp.float32,
         )
-        found.append((summed[:heads] + summed[heads:], largest, total))
-        for j in range(per_chunk):
-            to = table[i * per_chunk + j]
-            outgoing[to, :block_len, :] = lat[i, j, :, :rank]
-            outgoing[to, block_len : 2 * block_len, :] = lat[i, j, :, rank:]
+        return (both[:heads] + both[heads:], largest, total)
+
+    scores, weights, found = ({}, {}, [])
+    for step in range(chunks + 2):
+        if step < chunks:
+            large[step].wait()
+            scores[step] = scored(step)
+        if 0 <= step - 1 < chunks:
+            weights[step - 1] = weighed(*scores.pop(step - 1))
+        if step >= 2:
+            found.append(summed(step - 2, *weights.pop(step - 2)))
     largest = found[0][1]
-    for _, other, _ in found[1:]:
-        largest = jnp.maximum(largest, other)
+    for chunk in found[1:]:
+        largest = jnp.maximum(largest, chunk[1])
     factors = [jnp.exp(f[1] - largest) for f in found]
     out[0] = sum(f[0] * k for f, k in zip(found, factors))
     out[1] = jnp.broadcast_to(largest, (heads, rank))
     out[2] = jnp.broadcast_to(sum(f[2] * k for f, k in zip(found, factors)), (heads, rank))
 
 
-def attend(latent, up_key, queries, lengths, block_dest, chunks, extra):
-    count, block_len, width = latent.shape
-    groups = up_key.shape[0]
-    _, q_heads, head_dim = queries.shape
-    heads = q_heads // groups
-    rank = width // 2
+def attend(latent, up_key, queries, lengths, chunks):
+    heads = queries.shape[1] // up_key.shape[0]
     return pl.pallas_call(
         attend_kernel,
         out_shape=(
-            jax.ShapeDtypeStruct((3, heads, rank), jnp.float32),
-            jax.ShapeDtypeStruct((count, 2 * block_len + extra, rank), latent.dtype),
+            jax.ShapeDtypeStruct((3, heads, latent.shape[2] // 2), jnp.float32),
+            jax.ShapeDtypeStruct(latent.shape, latent.dtype),
         ),
-        in_specs=[HBM] * 5,
-        out_specs=(VMEM, VMEM),
+        in_specs=[HBM] * 4,
+        out_specs=(VMEM,) * 2,
         scratch_shapes=[
-            pltpu.VMEM((chunks, count // chunks, block_len, width), latent.dtype),
             pltpu.VMEM(up_key.shape[1:], up_key.dtype),
-            pltpu.VMEM((heads, head_dim), queries.dtype),
-            pltpu.SMEM((count,), jnp.int32),
+            pltpu.VMEM((heads, queries.shape[2]), queries.dtype),
             pltpu.SMEM(lengths.shape, jnp.int32),
-            pltpu.SemaphoreType.DMA((4 + chunks,)),
+            pltpu.SemaphoreType.DMA((3 + chunks,)),
         ],
         compiler_params=PARAMS,
         name="attend",
-    )(lengths, block_dest, latent, up_key, queries)
+    )(*[in_hbm(x) for x in (lengths, latent, up_key, queries)])
+
+
+def in_hbm(x):
+    return pltpu.with_memory_space_constraint(x, pltpu.HBM)
+
+
+def slot_kernel(dests, lat, after, outgoing, table, sem):
+    count, block_len, width = lat.shape
+    rank = width // 2
+    first = pl.multiple_of(lax.axis_index(SEQ) * count, count)
+    copy = pltpu.make_async_copy(dests.at[pl.ds(first, count)], table, sem)
+    copy.start()
+    copy.wait()
+    for b in range(count):
+        to = table[b]
+        outgoing[to, :block_len, :] = lat[b, :, :rank]
+        outgoing[to, block_len : 2 * block_len, :] = lat[b, :, rank:]
+
+
+def slot(block_dest, lat, after, extra):
+    count, block_len, width = lat.shape
+    return pl.pallas_call(
+        slot_kernel,
+        out_shape=jax.ShapeDtypeStruct((count, 2 * block_len + extra, width // 2), lat.dtype),
+        in_specs=[HBM, VMEM, VMEM],
+        out_specs=VMEM,
+        scratch_shapes=[pltpu.SMEM((count,), jnp.int32), pltpu.SemaphoreType.DMA],
+        compiler_params=PARAMS,
+        name="slot",
+    )(in_hbm(block_dest), lat, after)
 
 
 def joined(first, second):
@@ -139,9 +167,13 @@
     return (accum, largest, first[2] * factor_a + second[2] * factor_b)
 
 
+def half_kept():
+    return (lax.axis_index("seq_2") + lax.axis_index("seq_1")) % 2
+
+
 def merge_kernel(mine, theirs, out):
     kept = out.shape[1]
-    rows = pl.ds(pl.multiple_of(lax.axis_index("seq_2") * kept, kept), kept)
+    rows = pl.ds(pl.multiple_of(half_kept() * kept, kept), kept)
     both = joined(
         [mine[i, rows, :] for i in range(3)], [theirs[i, rows, :] for i in range(3)]
     )
@@ -168,7 +200,7 @@
     mean = jnp.where(lax.axis_index("seq_1") % 2 == 1, mean[half:], mean[:half])
     value_map = up_value[lax.axis_index("grp")]
     value_map = jnp.where(
-        lax.axis_index("seq_2") == 1, value_map[:, head_dim:], value_map[:, :head_dim]
+        half_kept() == 1, value_map[:, head_dim:], value_map[:, :head_dim]
     )
     wide = lax.dot_general(
         split(mean, 3), value_map, (((1,), (0,)), ((), ())), preferred_element_type=jnp.float32
@@ -214,7 +246,7 @@
             seq = 2 * x + y // 2
             part = received[g * shards + s, 2 * block_len :, :].astype(jnp.float32)
             part = part[half:] + part[:half]
-            first = g * 16 + c * 8 + y % 2 * 4
+            first = g * 16 + (c + y) % 2 * 8 + y % 2 * 4
             for j in range(half):
                 at = (first + j) * rank
                 rows_out[seq : seq + 1, at : at + rank] = part[j : j + 1]
@@ -250,17 +282,18 @@
     )(received)
 
 
-def swap(x, axis, mask):
-    return lax.ppermute(x, axis, [(i, i ^ mask) for i in range(lax.axis_size(axis))])
+def swap(x, axes, mask):
+    return lax.ppermute(x, axes, [(i, i ^ mask) for i in range(lax.axis_size(axes))])
 
 
 def body(latent, up_key, up_value, queries, lengths, block_dest):
     groups = up_key.shape[0]
     block_len = latent.shape[2]
     batch, q_heads, _ = queries.shape
-    part, outgoing = attend(latent[0], up_key, queries, lengths, block_dest, 4, 8)
+    part, lat = attend(latent[0], up_key, queries, lengths, 2)
     part = merge(part, swap(part, "seq_2", 1))
-    outgoing = pack(part, swap(part, "seq_1", 1), up_value, outgoing)
+    outgoing = slot(block_dest, lat, part, 8)
+    outgoing = pack(part, swap(part, ("seq_1", "seq_2"), 3), up_value, outgoing)
     received = lax.all_to_all(outgoing, GRP_SEQ, split_axis=0, concat_axis=0, tiled=True)
     return unpack(received, groups, batch, q_heads, block_len)
 

time: 59.7 us -> 53.4 us (0.89)
  local copies, waits for them, and re-layouts: 4.81 us -> 0.01 us
  waiting for transfers between devices: 3.19 us -> 1.84 us
    unnamed x12 -> x2, local copies, waits for them, and re-layouts: 4.81 us -> 0.01 us
    ppermute x2, waiting for transfers between devices: 3.19 us -> 1.84 us  [swap(): lax.ppermute(x, axes, [(i, i ^ mask) for i in range(lax.axis_size(axes))])]
    pallas_call x0 -> x1, Pallas kernels: none -> 1.04 us  [slot(): pl.pallas_call(slot_kernel, out_shape=jax.ShapeDtypeStruct((count, 2 * bl...]
    pallas_call x1, Pallas kernels: 3 us -> 2.23 us  [attend(): pl.pallas_call(attend_kernel, out_shape=(jax.ShapeDtypeStruct((3, heads,...]
  transfers between devices with their start and end apart: 2 -> 2, of which waited for: 2 -> 2; matrix products, arithmetic and copies ran while one was open for 0% -> 0% of each run, Pallas kernels for 0% -> 2%
where the time goes in v6:
time: 53.4 us; the launch traced here: 53.2 us
  blocking collectives  44.1 us (83%)
  Pallas kernels  4.96 us (9%)
  waiting for transfers between devices  1.84 us (3%)
  starting transfers between devices  1.58 us (3%)
  between operations  0.67 us (1%)
    all_to_all x1, blocking collectives, body(): lax.all_to_all(outgoing, GRP_SEQ, split_axis=0, concat_axis=0, tiled=True)  44.1 us
    pallas_call x1, Pallas kernels, attend(): pl.pallas_call(attend_kernel, out_shape=(jax.ShapeDtypeStruct((3, heads,...  2.23 us
    ppermute x2, waiting for transfers between devices, swap(): lax.ppermute(x, axes, [(i, i ^ mask) for i in range(lax.axis_size(axes))])  1.84 us
    ppermute x2, starting transfers between devices, swap(): lax.ppermute(x, axes, [(i, i ^ mask) for i in range(lax.axis_size(axes))])  1.58 us
    pallas_call x1, Pallas kernels, unpack(): pl.pallas_call(unpack_kernel, out_shape=(jax.ShapeDtypeStruct((1, groups,...  1.48 us
  transfers between devices with their start and end apart: 2, of which 2 were waited for; matrix products, arithmetic and copies ran while one was open for 0% of the time, Pallas kernels for 2%

profile of v6, /device:TPU:0, one launch (start us, length us, event | category | flops | bytes accessed | tf_op | source)
XLA Modules:
  0.0 53.2 jit_solution(7572780227640389279)
XLA Ops:
  0.6 2.2 %attend.1 = (f32[3,16,128]{2,1,0:T(8,128)S(1)}, bf16[128,32,256]{2,1,0:T(8,128)(2,1)S(1)}) custom-call(s32[8]{0:T(128)} %ends.1, bf16[128,32,256]{2,1,0:T(8,128)(2,1)} %bitcast.1, bf16[4,128,256]{2,1,0:T(8,128)(2,1)} %up_key.1, bf16[8,64,128]{2,1,0:T(8,128)(2,1)} %queries.1), custom_call_target="tpu_custom_call" | custom-call | tf_op jit(solution)/shard_map/attend/pallas_call | solution.py:113
  2.9 0.0 copy-start
  2.9 0.1 collective-permute-start
  3.0 1.2 %collective-permute-done.theirs = f32[3,16,128]{2,1,0:T(8,128)S(1)} collective-permute-done((f32[3,16,128]{2,1,0:T(8,128)S(1)}, f32[3,16,128]{2,1,0:T(8,128)S(1)}, u32[]{:S(2)}, u32[]{:S(2)}) %collective-permute-start) | collective-permute-done | bytes 24608 | tf_op jit(solution)/shard_map/ppermute | solution.py:286
  4.2 1.5 %collective-permute-start.1 = (f32[3,8,128]{2,1,0:T(8,128)S(1)}, f32[3,8,128]{2,1,0:T(8,128)S(1)}, u32[]{:S(2)}, u32[]{:S(2)}) collective-permute-start(f32[3,8,128]{2,1,0:T(8,128)S(1)} %merge.1.after.mine), channel_id=1, source_target_pairs={{0,3},{1,2},{2,1},{3,0},{4,7},{5,6},{6,5},{7,4},{8,11},{9,10},{10,... | collective-permute-start | bytes 36872 | tf_op jit(solution)/shard_map/ppermute | solution.py:286
  5.7 1.0 %slot.1._ = bf16[128,72,128]{2,1,0:T(8,128)(2,1)S(1)} custom-call(s32[4096]{0:T(1024)} %dests.1, bf16[128,32,256]{2,1,0:T(8,128)(2,1)S(1)} %get-tuple-element.5.lat, f32[3,8,128]{2,1,0:T(8,128)S(1)} %merge.1.after.mine), custom_call_target="tpu_custom_call" | custom-call | tf_op jit(solution)/shard_map/slot/pallas_call | solution.py:151
  6.7 0.7 %collective-permute-done.1.theirs = f32[3,8,128]{2,1,0:T(8,128)S(1)} collective-permute-done((f32[3,8,128]{2,1,0:T(8,128)S(1)}, f32[3,8,128]{2,1,0:T(8,128)S(1)}, u32[]{:S(2)}, u32[]{:S(2)}) %collective-permute-start.1) | collective-permute-done | bytes 12320 | tf_op jit(solution)/shard_map/ppermute | solution.py:286
  7.4 0.0 copy-done
  7.4 0.2 pack.1
  7.6 44.1 %all_to_all.5.received = bf16[128,72,128]{2,1,0:T(8,128)(2,1)S(1)} all-to-all(bf16[128,72,128]{2,1,0:T(8,128)(2,1)S(1)} %pack.1), channel_id=1, replica_groups=mesh['grp'=4,'seq_0'=4,'seq_1'=4,'seq_2'=2] {'grp','seq_0','seq_1','seq_2'}, dimensions={0} | all-to-all | bytes 4718592 | tf_op jit(solution)/shard_map/all_to_all | solution.py:297
  51.7 1.5 %unpack.1 = (bf16[1,4,32,32,256]{4,3,2,1,0:T(8,128)(2,1)}, f32[8,8192]{1,0:T(8,128)}) custom-call(bf16[128,72,128]{2,1,0:T(8,128)(2,1)S(1)} %all_to_all.5.received), custom_call_target="tpu_custom_call" | custom-call | tf_op jit(solution)/shard_map/unpack/pallas_call | solution.py:265
  (1 shorter events, 0.0 us)
Async XLA Ops:
  2.9 4.5 %copy-start = (bf16[4,128,256]{2,1,0:T(8,128)(2,1)S(1)}, bf16[4,128,256]{2,1,0:T(8,128)(2,1)}, u32[]{:S(2)}) copy-start(bf16[4,128,256]{2,1,0:T(8,128)(2,1)} %up_value.1) | copy-start | bytes 786436
  2.9 1.3 %collective-permute-start = (f32[3,16,128]{2,1,0:T(8,128)S(1)}, f32[3,16,128]{2,1,0:T(8,128)S(1)}, u32[]{:S(2)}, u32[]{:S(2)}) collective-permute-start(f32[3,16,128]{2,1,0:T(8,128)S(1)} %get-tuple-element.4.mine), channel_id=1, source_target_pairs={{0,1},{1,0},{2,3},{3,2},{4,5},{5,4},{6,7},{7,6},{8,9},{9,8},{10,11... | collective-permute-start | bytes 73736 | tf_op jit(solution)/shard_map/ppermute | solution.py:286
  4.2 3.2 %collective-permute-start.1 = (f32[3,8,128]{2,1,0:T(8,128)S(1)}, f32[3,8,128]{2,1,0:T(8,128)S(1)}, u32[]{:S(2)}, u32[]{:S(2)}) collective-permute-start(f32[3,8,128]{2,1,0:T(8,128)S(1)} %merge.1.after.mine), channel_id=1, source_target_pairs={{0,3},{1,2},{2,1},{3,0},{4,7},{5,6},{6,5},{7,4},{8,11},{9,10},{10,... | collective-permute-start | bytes 36872 | tf_op jit(solution)/shard_map/ppermute | solution.py:286

commit v7 on v6

--- a/solution.py
+++ b/solution.py
@@ -8,6 +8,7 @@
 
 SEQ = ("seq_0", "seq_1", "seq_2")
 GRP_SEQ = ("grp", "seq_0", "seq_1", "seq_2")
+EXCHANGE = ("seq_2", "grp", "seq_0", "seq_1")
 NEG = -1e30
 VMEM = pl.BlockSpec(memory_space=pltpu.VMEM)
 HBM = pl.BlockSpec(memory_space=pltpu.HBM)
@@ -141,7 +142,7 @@
     copy.start()
     copy.wait()
     for b in range(count):
-        to = table[b]
+        to = (table[b] & 1) * (count // 2) + (table[b] >> 1)
         outgoing[to, :block_len, :] = lat[b, :, :rank]
         outgoing[to, block_len : 2 * block_len, :] = lat[b, :, rank:]
 
@@ -225,26 +226,30 @@
 
 def unpack_kernel(received, decode, attended, rows_out, sems, row_sems):
     sources, rows, rank = received.shape
-    _, groups, shards, block_len, _ = decode.shape
+    _, groups, chips, cores, block_len, _ = decode.shape
     copies = []
     for g in range(groups):
-        for k in range(2):
-            copies.append(
-                pltpu.make_async_copy(
-                    received.at[pl.ds(g * shards, shards), pl.ds(k * block_len, block_len), :],
-                    decode.at[0, g, :, :, pl.ds(k * rank, rank)],
-                    sems.at[g, k],
+        for c in range(cores):
+            for k in range(2):
+                sent = pl.ds((c * groups + g) * chips, chips)
+                copies.append(
+                    pltpu.make_async_copy(
+                        received.at[sent, pl.ds(k * block_len, block_len), :],
+                        decode.at[0, g, :, c, :, pl.ds(k * rank, rank)],
+                        sems.at[g, c, k],
+                    )
                 )
-            )
     for c in copies:
         c.start()
     half = (rows - 2 * block_len) // 2
     span = rows_out.shape[1] // groups
     for g in range(groups):
-        for s in range(shards):
-            x, y, c = s // 8, s // 2 % 4, s % 2
+        for s in range(chips * cores):
+            chip, c = s // cores, s % cores
+            x, y = chip // 4, chip % 4
             seq = 2 * x + y // 2
-            part = received[g * shards + s, 2 * block_len :, :].astype(jnp.float32)
+            part = received[(c * groups + g) * chips + chip, 2 * block_len :, :]
+            part = part.astype(jnp.float32)
             part = part[half:] + part[:half]
             first = g * 16 + (c + y) % 2 * 8 + y % 2 * 4
             for j in range(half):
@@ -266,7 +271,7 @@
         unpack_kernel,
         out_shape=(
             jax.ShapeDtypeStruct(
-                (1, groups, sources // groups, block_len, 2 * rank), received.dtype
+                (1, groups, sources // groups // 2, 2, block_len, 2 * rank), received.dtype
             ),
             jax.ShapeDtypeStruct((batch, heads * rank), jnp.float32),
         ),
@@ -274,7 +279,7 @@
         out_specs=(HBM, HBM),
         scratch_shapes=[
             pltpu.VMEM((batch, heads * rank), jnp.float32),
-            pltpu.SemaphoreType.DMA((groups, 2)),
+            pltpu.SemaphoreType.DMA((groups, 2, 2)),
             pltpu.SemaphoreType.DMA((groups,)),
         ],
         compiler_params=PARAMS,
@@ -294,8 +299,9 @@
     part = merge(part, swap(part, "seq_2", 1))
     outgoing = slot(block_dest, lat, part, 8)
     outgoing = pack(part, swap(part, ("seq_1", "seq_2"), 3), up_value, outgoing)
-    received = lax.all_to_all(outgoing, GRP_SEQ, split_axis=0, concat_axis=0, tiled=True)
-    return unpack(received, groups, batch, q_heads, block_len)
+    received = lax.all_to_all(outgoing, EXCHANGE, split_axis=0, concat_axis=0, tiled=True)
+    decode, attended = unpack(received, groups, batch, q_heads, block_len)
+    return (decode.reshape(1, groups, -1, *latent.shape[2:]), attended)
 
 
 def solution(mesh):

time: 53.4 us -> 52.2 us (0.978); the launches traced: 53.2 us -> 51.3 us
  blocking collectives: 44.1 us -> 42.2 us
    all_to_all x1, blocking collectives: 44.1 us -> 42.2 us  [body(): lax.all_to_all(outgoing, EXCHANGE, split_axis=0, concat_axis=0, tiled=True)]
where the time goes in v7:
time: 52.2 us; the launch traced here: 51.3 us
  blocking collectives  42.2 us (81%)
  Pallas kernels  5.07 us (10%)
  waiting for transfers between devices  1.79 us (3%)
  starting transfers between devices  1.58 us (3%)
  between operations  0.67 us (1%)
    all_to_all x1, blocking collectives, body(): lax.all_to_all(outgoing, EXCHANGE, split_axis=0, concat_axis=0, tiled=True)  42.2 us
    pallas_call x1, Pallas kernels, attend(): pl.pallas_call(attend_kernel, out_shape=(jax.ShapeDtypeStruct((3, heads,...  2.23 us
    ppermute x2, waiting for transfers between devices, swap(): lax.ppermute(x, axes, [(i, i ^ mask) for i in range(lax.axis_size(axes))])  1.79 us
    ppermute x2, starting transfers between devices, swap(): lax.ppermute(x, axes, [(i, i ^ mask) for i in range(lax.axis_size(axes))])  1.58 us
    pallas_call x1, Pallas kernels, unpack(): pl.pallas_call(unpack_kernel, out_shape=(jax.ShapeDtypeStruct((1, groups,...  1.55 us
    pallas_call x1, Pallas kernels, slot(): pl.pallas_call(slot_kernel, out_shape=jax.ShapeDtypeStruct((count, 2 * bl...  1.09 us
  transfers between devices with their start and end apart: 2, of which 2 were waited for; matrix products, arithmetic and copies ran while one was open for 0% of the time, Pallas kernels for 2%

profile of v7, /device:TPU:0, one launch (start us, length us, event | category | flops | bytes accessed | tf_op | source)
XLA Modules:
  0.0 51.3 jit_solution(16994222153892480233)
XLA Ops:
  0.6 2.2 %attend.1 = (f32[3,16,128]{2,1,0:T(8,128)S(1)}, bf16[128,32,256]{2,1,0:T(8,128)(2,1)S(1)}) custom-call(s32[8]{0:T(128)} %ends.1, bf16[128,32,256]{2,1,0:T(8,128)(2,1)} %bitcast.2, bf16[4,128,256]{2,1,0:T(8,128)(2,1)} %up_key.1, bf16[8,64,128]{2,1,0:T(8,128)(2,1)} %queries.1), custom_call_target="tpu_custom_call" | custom-call | tf_op jit(solution)/shard_map/attend/pallas_call | solution.py:114
  2.9 0.0 copy-start
  2.9 0.1 collective-permute-start
  3.0 1.2 %collective-permute-done.theirs = f32[3,16,128]{2,1,0:T(8,128)S(1)} collective-permute-done((f32[3,16,128]{2,1,0:T(8,128)S(1)}, f32[3,16,128]{2,1,0:T(8,128)S(1)}, u32[]{:S(2)}, u32[]{:S(2)}) %collective-permute-start) | collective-permute-done | bytes 24608 | tf_op jit(solution)/shard_map/ppermute | solution.py:291
  4.2 1.5 %collective-permute-start.1 = (f32[3,8,128]{2,1,0:T(8,128)S(1)}, f32[3,8,128]{2,1,0:T(8,128)S(1)}, u32[]{:S(2)}, u32[]{:S(2)}) collective-permute-start(f32[3,8,128]{2,1,0:T(8,128)S(1)} %merge.1.after.mine), channel_id=1, source_target_pairs={{0,3},{1,2},{2,1},{3,0},{4,7},{5,6},{6,5},{7,4},{8,11},{9,10},{10,... | collective-permute-start | bytes 36872 | tf_op jit(solution)/shard_map/ppermute | solution.py:291
  5.7 1.1 %slot.1._ = bf16[128,72,128]{2,1,0:T(8,128)(2,1)S(1)} custom-call(s32[4096]{0:T(1024)} %dests.1, bf16[128,32,256]{2,1,0:T(8,128)(2,1)S(1)} %get-tuple-element.7.lat, f32[3,8,128]{2,1,0:T(8,128)S(1)} %merge.1.after.mine), custom_call_target="tpu_custom_call" | custom-call | tf_op jit(solution)/shard_map/slot/pallas_call | solution.py:152
  6.8 0.6 %collective-permute-done.1.theirs = f32[3,8,128]{2,1,0:T(8,128)S(1)} collective-permute-done((f32[3,8,128]{2,1,0:T(8,128)S(1)}, f32[3,8,128]{2,1,0:T(8,128)S(1)}, u32[]{:S(2)}, u32[]{:S(2)}) %collective-permute-start.1) | collective-permute-done | bytes 12320 | tf_op jit(solution)/shard_map/ppermute | solution.py:291
  7.4 0.0 copy-done
  7.4 0.2 pack.1
  7.6 42.2 %all_to_all.5.received = bf16[128,72,128]{2,1,0:T(8,128)(2,1)S(1)} all-to-all(bf16[128,72,128]{2,1,0:T(8,128)(2,1)S(1)} %pack.1), channel_id=1, replica_groups=mesh['grp'=4,'seq_0'=4,'seq_1'=4,'seq_2'=2] {'seq_2','grp','seq_0','seq_1'}, dimensions={0} | all-to-all | bytes 4718592 | tf_op jit(solution)/shard_map/all_to_all | solution.py:302
  49.8 1.6 %unpack.1 = (bf16[1,4,16,2,32,256]{5,4,3,2,1,0:T(8,128)(2,1)}, f32[8,8192]{1,0:T(8,128)}) custom-call(bf16[128,72,128]{2,1,0:T(8,128)(2,1)S(1)} %all_to_all.5.received), custom_call_target="tpu_custom_call" | custom-call | tf_op jit(solution)/shard_map/unpack/pallas_call | solution.py:270
  (1 shorter events, 0.0 us)
Async XLA Ops:
  2.9 4.5 %copy-start = (bf16[4,128,256]{2,1,0:T(8,128)(2,1)S(1)}, bf16[4,128,256]{2,1,0:T(8,128)(2,1)}, u32[]{:S(2)}) copy-start(bf16[4,128,256]{2,1,0:T(8,128)(2,1)} %up_value.1) | copy-start | bytes 786436
  2.9 1.3 %collective-permute-start = (f32[3,16,128]{2,1,0:T(8,128)S(1)}, f32[3,16,128]{2,1,0:T(8,128)S(1)}, u32[]{:S(2)}, u32[]{:S(2)}) collective-permute-start(f32[3,16,128]{2,1,0:T(8,128)S(1)} %get-tuple-element.6.mine), channel_id=1, source_target_pairs={{0,1},{1,0},{2,3},{3,2},{4,5},{5,4},{6,7},{7,6},{8,9},{9,8},{10,11... | collective-permute-start | bytes 73736 | tf_op jit(solution)/shard_map/ppermute | solution.py:291
  4.2 3.2 %collective-permute-start.1 = (f32[3,8,128]{2,1,0:T(8,128)S(1)}, f32[3,8,128]{2,1,0:T(8,128)S(1)}, u32[]{:S(2)}, u32[]{:S(2)}) collective-permute-start(f32[3,8,128]{2,1,0:T(8,128)S(1)} %merge.1.after.mine), channel_id=1, source_target_pairs={{0,3},{1,2},{2,1},{3,0},{4,7},{5,6},{6,5},{7,4},{8,11},{9,10},{10,... | collective-permute-start | bytes 36872 | tf_op jit(solution)/shard_map/ppermute | solution.py:291

commit v8 on v7

--- a/solution.py
+++ b/solution.py
@@ -221,7 +221,7 @@
         input_output_aliases={3: 0},
         compiler_params=PARAMS,
         name="pack",
-    )(mine, theirs, up_value, outgoing)
+    )(mine, theirs, up_value, pltpu.with_memory_space_constraint(outgoing, pltpu.VMEM))
 
 
 def unpack_kernel(received, decode, attended, rows_out, sems, row_sems):

time: 52.2 us -> 52.2 us (level)
  no operation moved by 1% of the time
where the time goes in v8:
time: 52.2 us; the launch traced here: 51.3 us
  blocking collectives  42.2 us (81%)
  Pallas kernels  5.07 us (10%)
  waiting for transfers between devices  1.79 us (3%)
  starting transfers between devices  1.58 us (3%)
  between operations  0.67 us (1%)
    all_to_all x1, blocking collectives, body(): lax.all_to_all(outgoing, EXCHANGE, split_axis=0, concat_axis=0, tiled=True)  42.2 us
    pallas_call x1, Pallas kernels, attend(): pl.pallas_call(attend_kernel, out_shape=(jax.ShapeDtypeStruct((3, heads,...  2.23 us
    ppermute x2, waiting for transfers between devices, swap(): lax.ppermute(x, axes, [(i, i ^ mask) for i in range(lax.axis_size(axes))])  1.79 us
    ppermute x2, starting transfers between devices, swap(): lax.ppermute(x, axes, [(i, i ^ mask) for i in range(lax.axis_size(axes))])  1.58 us
    pallas_call x1, Pallas kernels, unpack(): pl.pallas_call(unpack_kernel, out_shape=(jax.ShapeDtypeStruct((1, groups,...  1.55 us
    pallas_call x1, Pallas kernels, slot(): pl.pallas_call(slot_kernel, out_shape=jax.ShapeDtypeStruct((count, 2 * bl...  1.09 us
  transfers between devices with their start and end apart: 2, of which 2 were waited for; matrix products, arithmetic and copies ran while one was open for 0% of the time, Pallas kernels for 2%

profile of v8, /device:TPU:0, one launch (start us, length us, event | category | flops | bytes accessed | tf_op | source)
XLA Modules:
  0.0 51.3 jit_solution(16994222153892480233)
XLA Ops:
  0.6 2.2 %attend.1 = (f32[3,16,128]{2,1,0:T(8,128)S(1)}, bf16[128,32,256]{2,1,0:T(8,128)(2,1)S(1)}) custom-call(s32[8]{0:T(128)} %ends.1, bf16[128,32,256]{2,1,0:T(8,128)(2,1)} %bitcast.2, bf16[4,128,256]{2,1,0:T(8,128)(2,1)} %up_key.1, bf16[8,64,128]{2,1,0:T(8,128)(2,1)} %queries.1), custom_call_target="tpu_custom_call" | custom-call | tf_op jit(solution)/shard_map/attend/pallas_call | solution.py:114
  2.9 0.0 copy-start
  2.9 0.1 collective-permute-start
  3.0 1.2 %collective-permute-done.theirs = f32[3,16,128]{2,1,0:T(8,128)S(1)} collective-permute-done((f32[3,16,128]{2,1,0:T(8,128)S(1)}, f32[3,16,128]{2,1,0:T(8,128)S(1)}, u32[]{:S(2)}, u32[]{:S(2)}) %collective-permute-start) | collective-permute-done | bytes 24608 | tf_op jit(solution)/shard_map/ppermute | solution.py:291
  4.2 1.5 %collective-permute-start.1 = (f32[3,8,128]{2,1,0:T(8,128)S(1)}, f32[3,8,128]{2,1,0:T(8,128)S(1)}, u32[]{:S(2)}, u32[]{:S(2)}) collective-permute-start(f32[3,8,128]{2,1,0:T(8,128)S(1)} %merge.1.after.mine), channel_id=1, source_target_pairs={{0,3},{1,2},{2,1},{3,0},{4,7},{5,6},{6,5},{7,4},{8,11},{9,10},{10,... | collective-permute-start | bytes 36872 | tf_op jit(solution)/shard_map/ppermute | solution.py:291
  5.7 1.1 %slot.1._ = bf16[128,72,128]{2,1,0:T(8,128)(2,1)S(1)} custom-call(s32[4096]{0:T(1024)} %dests.1, bf16[128,32,256]{2,1,0:T(8,128)(2,1)S(1)} %get-tuple-element.7.lat, f32[3,8,128]{2,1,0:T(8,128)S(1)} %merge.1.after.mine), custom_call_target="tpu_custom_call" | custom-call | tf_op jit(solution)/shard_map/slot/pallas_call | solution.py:152
  6.8 0.6 %collective-permute-done.1.theirs = f32[3,8,128]{2,1,0:T(8,128)S(1)} collective-permute-done((f32[3,8,128]{2,1,0:T(8,128)S(1)}, f32[3,8,128]{2,1,0:T(8,128)S(1)}, u32[]{:S(2)}, u32[]{:S(2)}) %collective-permute-start.1) | collective-permute-done | bytes 12320 | tf_op jit(solution)/shard_map/ppermute | solution.py:291
  7.4 0.0 copy-done
  7.4 0.2 pack.1
  7.6 42.2 %all_to_all.5.received = bf16[128,72,128]{2,1,0:T(8,128)(2,1)S(1)} all-to-all(bf16[128,72,128]{2,1,0:T(8,128)(2,1)S(1)} %pack.1), channel_id=1, replica_groups=mesh['grp'=4,'seq_0'=4,'seq_1'=4,'seq_2'=2] {'seq_2','grp','seq_0','seq_1'}, dimensions={0} | all-to-all | bytes 4718592 | tf_op jit(solution)/shard_map/all_to_all | solution.py:302
  49.8 1.6 %unpack.1 = (bf16[1,4,16,2,32,256]{5,4,3,2,1,0:T(8,128)(2,1)}, f32[8,8192]{1,0:T(8,128)}) custom-call(bf16[128,72,128]{2,1,0:T(8,128)(2,1)S(1)} %all_to_all.5.received), custom_call_target="tpu_custom_call" | custom-call | tf_op jit(solution)/shard_map/unpack/pallas_call | solution.py:270
  (1 shorter events, 0.0 us)
Async XLA Ops:
  2.9 4.5 %copy-start = (bf16[4,128,256]{2,1,0:T(8,128)(2,1)S(1)}, bf16[4,128,256]{2,1,0:T(8,128)(2,1)}, u32[]{:S(2)}) copy-start(bf16[4,128,256]{2,1,0:T(8,128)(2,1)} %up_value.1) | copy-start | bytes 786436
  2.9 1.3 %collective-permute-start = (f32[3,16,128]{2,1,0:T(8,128)S(1)}, f32[3,16,128]{2,1,0:T(8,128)S(1)}, u32[]{:S(2)}, u32[]{:S(2)}) collective-permute-start(f32[3,16,128]{2,1,0:T(8,128)S(1)} %get-tuple-element.6.mine), channel_id=1, source_target_pairs={{0,1},{1,0},{2,3},{3,2},{4,5},{5,4},{6,7},{7,6},{8,9},{9,8},{10,11... | collective-permute-start | bytes 73736 | tf_op jit(solution)/shard_map/ppermute | solution.py:291
  4.2 3.2 %collective-permute-start.1 = (f32[3,8,128]{2,1,0:T(8,128)S(1)}, f32[3,8,128]{2,1,0:T(8,128)S(1)}, u32[]{:S(2)}, u32[]{:S(2)}) collective-permute-start(f32[3,8,128]{2,1,0:T(8,128)S(1)} %merge.1.after.mine), channel_id=1, source_target_pairs={{0,3},{1,2},{2,1},{3,0},{4,7},{5,6},{6,5},{7,4},{8,11},{9,10},{10,... | collective-permute-start | bytes 36872 | tf_op jit(solution)/shard_map/ppermute | solution.py:291

commit v9 on v8

--- a/solution.py
+++ b/solution.py
@@ -8,7 +8,7 @@
 
 SEQ = ("seq_0", "seq_1", "seq_2")
 GRP_SEQ = ("grp", "seq_0", "seq_1", "seq_2")
-EXCHANGE = ("seq_2", "grp", "seq_0", "seq_1")
+EXCHANGE = ("seq_2", "grp", "seq_1", "seq_0")
 NEG = -1e30
 VMEM = pl.BlockSpec(memory_space=pltpu.VMEM)
 HBM = pl.BlockSpec(memory_space=pltpu.HBM)
@@ -142,7 +142,8 @@
     copy.start()
     copy.wait()
     for b in range(count):
-        to = (table[b] & 1) * (count // 2) + (table[b] >> 1)
+        d = table[b]
+        to = (d & 1) * 64 + (d >> 5) * 16 + ((d >> 1) & 3) * 4 + ((d >> 3) & 3)
         outgoing[to, :block_len, :] = lat[b, :, :rank]
         outgoing[to, block_len : 2 * block_len, :] = lat[b, :, rank:]
 
@@ -225,18 +226,17 @@
 
 
 def unpack_kernel(received, decode, attended, rows_out, sems, row_sems):
-    sources, rows, rank = received.shape
-    _, groups, chips, cores, block_len, _ = decode.shape
+    cores, groups, high, wide, rows, rank = received.shape
+    block_len = decode.shape[5]
     copies = []
-    for g in range(groups):
-        for c in range(cores):
+    for c in range(cores):
+        for y in range(high):
             for k in range(2):
-                sent = pl.ds((c * groups + g) * chips, chips)
                 copies.append(
                     pltpu.make_async_copy(
-                        received.at[sent, pl.ds(k * block_len, block_len), :],
-                        decode.at[0, g, :, c, :, pl.ds(k * rank, rank)],
-                        sems.at[g, c, k],
+                        received.at[c, :, y, :, pl.ds(k * block_len, block_len), :],
+                        decode.at[0, :, :, y, c, :, pl.ds(k * rank, rank)],
+                        sems.at[c, y, k],
                     )
                 )
     for c in copies:
@@ -244,11 +244,10 @@
     half = (rows - 2 * block_len) // 2
     span = rows_out.shape[1] // groups
     for g in range(groups):
-        for s in range(chips * cores):
-            chip, c = s // cores, s % cores
-            x, y = chip // 4, chip % 4
+        for s in range(wide * high * cores):
+            x, y, c = s // (high * cores), s // cores % high, s % cores
             seq = 2 * x + y // 2
-            part = received[(c * groups + g) * chips + chip, 2 * block_len :, :]
+            part = received[c, g, y, x, 2 * block_len :, :]
             part = part.astype(jnp.float32)
             part = part[half:] + part[:half]
             first = g * 16 + (c + y) % 2 * 8 + y % 2 * 4
@@ -266,12 +265,13 @@
 
 
 def unpack(received, groups, batch, heads, block_len):
-    sources, _, rank = received.shape
+    _, rows, rank = received.shape
+    received = received.reshape(2, groups, 4, 4, rows, rank)
     return pl.pallas_call(
         unpack_kernel,
         out_shape=(
             jax.ShapeDtypeStruct(
-                (1, groups, sources // groups // 2, 2, block_len, 2 * rank), received.dtype
+                (1, groups, 4, 4, 2, block_len, 2 * rank), received.dtype
             ),
             jax.ShapeDtypeStruct((batch, heads * rank), jnp.float32),
         ),
@@ -279,7 +279,7 @@
         out_specs=(HBM, HBM),
         scratch_shapes=[
             pltpu.VMEM((batch, heads * rank), jnp.float32),
-            pltpu.SemaphoreType.DMA((groups, 2, 2)),
+            pltpu.SemaphoreType.DMA((2, 4, 2)),
             pltpu.SemaphoreType.DMA((groups,)),
         ],
         compiler_params=PARAMS,

time: 52.2 us -> 51.9 us (level)
  no operation moved by 1% of the time
where the time goes in v9:
time: 51.9 us; the launch traced here: 51.4 us
  blocking collectives  42.3 us (82%)
  Pallas kernels  5.17 us (10%)
  waiting for transfers between devices  1.7 us (3%)
  starting transfers between devices  1.58 us (3%)
  between operations  0.67 us (1%)
    all_to_all x1, blocking collectives, body(): lax.all_to_all(outgoing, EXCHANGE, split_axis=0, concat_axis=0, tiled=True)  42.3 us
    pallas_call x1, Pallas kernels, attend(): pl.pallas_call(attend_kernel, out_shape=(jax.ShapeDtypeStruct((3, heads,...  2.23 us
    ppermute x2, waiting for transfers between devices, swap(): lax.ppermute(x, axes, [(i, i ^ mask) for i in range(lax.axis_size(axes))])  1.7 us
    ppermute x2, starting transfers between devices, swap(): lax.ppermute(x, axes, [(i, i ^ mask) for i in range(lax.axis_size(axes))])  1.58 us
    pallas_call x1, Pallas kernels, unpack(): pl.pallas_call(unpack_kernel, out_shape=(jax.ShapeDtypeStruct((1, groups,...  1.55 us
    pallas_call x1, Pallas kernels, slot(): pl.pallas_call(slot_kernel, out_shape=jax.ShapeDtypeStruct((count, 2 * bl...  1.18 us
  transfers between devices with their start and end apart: 2, of which 2 were waited for; matrix products, arithmetic and copies ran while one was open for 0% of the time, Pallas kernels for 2%

profile of v9, /device:TPU:0, one launch (start us, length us, event | category | flops | bytes accessed | tf_op | source)
XLA Modules:
  0.0 51.4 jit_solution(7243310698017269936)
XLA Ops:
  0.6 2.2 %attend.1 = (f32[3,16,128]{2,1,0:T(8,128)S(1)}, bf16[128,32,256]{2,1,0:T(8,128)(2,1)S(1)}) custom-call(s32[8]{0:T(128)} %ends.1, bf16[128,32,256]{2,1,0:T(8,128)(2,1)} %bitcast.4, bf16[4,128,256]{2,1,0:T(8,128)(2,1)} %up_key.1, bf16[8,64,128]{2,1,0:T(8,128)(2,1)} %queries.1), custom_call_target="tpu_custom_call" | custom-call | tf_op jit(solution)/shard_map/attend/pallas_call | solution.py:114
  2.9 0.0 copy-start
  2.9 0.1 collective-permute-start
  3.0 1.2 %collective-permute-done.theirs = f32[3,16,128]{2,1,0:T(8,128)S(1)} collective-permute-done((f32[3,16,128]{2,1,0:T(8,128)S(1)}, f32[3,16,128]{2,1,0:T(8,128)S(1)}, u32[]{:S(2)}, u32[]{:S(2)}) %collective-permute-start) | collective-permute-done | bytes 24608 | tf_op jit(solution)/shard_map/ppermute | solution.py:291
  4.2 1.5 %collective-permute-start.1 = (f32[3,8,128]{2,1,0:T(8,128)S(1)}, f32[3,8,128]{2,1,0:T(8,128)S(1)}, u32[]{:S(2)}, u32[]{:S(2)}) collective-permute-start(f32[3,8,128]{2,1,0:T(8,128)S(1)} %merge.1.after.mine), channel_id=1, source_target_pairs={{0,3},{1,2},{2,1},{3,0},{4,7},{5,6},{6,5},{7,4},{8,11},{9,10},{10,... | collective-permute-start | bytes 36872 | tf_op jit(solution)/shard_map/ppermute | solution.py:291
  5.7 1.2 %slot.1._ = bf16[128,72,128]{2,1,0:T(8,128)(2,1)S(1)} custom-call(s32[4096]{0:T(1024)} %dests.1, bf16[128,32,256]{2,1,0:T(8,128)(2,1)S(1)} %get-tuple-element.7.lat, f32[3,8,128]{2,1,0:T(8,128)S(1)} %merge.1.after.mine), custom_call_target="tpu_custom_call" | custom-call | tf_op jit(solution)/shard_map/slot/pallas_call | solution.py:153
  6.9 0.5 %collective-permute-done.1.theirs = f32[3,8,128]{2,1,0:T(8,128)S(1)} collective-permute-done((f32[3,8,128]{2,1,0:T(8,128)S(1)}, f32[3,8,128]{2,1,0:T(8,128)S(1)}, u32[]{:S(2)}, u32[]{:S(2)}) %collective-permute-start.1) | collective-permute-done | bytes 12320 | tf_op jit(solution)/shard_map/ppermute | solution.py:291
  7.4 0.0 copy-done
  7.4 0.2 pack.1
  7.6 42.3 %all_to_all.5 = bf16[128,72,128]{2,1,0:T(8,128)(2,1)S(1)} all-to-all(bf16[128,72,128]{2,1,0:T(8,128)(2,1)S(1)} %pack.1), channel_id=1, replica_groups=mesh['grp'=4,'seq_0'=4,'seq_1'=4,'seq_2'=2] {'seq_2','grp','seq_1','seq_0'}, dimensions={0} | all-to-all | bytes 4718592 | tf_op jit(solution)/shard_map/all_to_all | solution.py:302
  49.9 1.6 %unpack.1 = (bf16[1,4,4,4,2,32,256]{6,5,4,3,2,1,0:T(8,128)(2,1)}, f32[8,8192]{1,0:T(8,128)}) custom-call(bf16[2,4,4,4,72,128]{5,4,3,2,1,0:T(8,128)(2,1)S(1)} %bitcast.3), custom_call_target="tpu_custom_call" | custom-call | tf_op jit(solution)/shard_map/unpack/pallas_call | solution.py:270
  (1 shorter events, 0.0 us)
Async XLA Ops:
  2.9 4.5 %copy-start = (bf16[4,128,256]{2,1,0:T(8,128)(2,1)S(1)}, bf16[4,128,256]{2,1,0:T(8,128)(2,1)}, u32[]{:S(2)}) copy-start(bf16[4,128,256]{2,1,0:T(8,128)(2,1)} %up_value.1) | copy-start | bytes 786436
  2.9 1.3 %collective-permute-start = (f32[3,16,128]{2,1,0:T(8,128)S(1)}, f32[3,16,128]{2,1,0:T(8,128)S(1)}, u32[]{:S(2)}, u32[]{:S(2)}) collective-permute-start(f32[3,16,128]{2,1,0:T(8,128)S(1)} %get-tuple-element.6.mine), channel_id=1, source_target_pairs={{0,1},{1,0},{2,3},{3,2},{4,5},{5,4},{6,7},{7,6},{8,9},{9,8},{10,11... | collective-permute-start | bytes 73736 | tf_op jit(solution)/shard_map/ppermute | solution.py:291
  4.2 3.2 %collective-permute-start.1 = (f32[3,8,128]{2,1,0:T(8,128)S(1)}, f32[3,8,128]{2,1,0:T(8,128)S(1)}, u32[]{:S(2)}, u32[]{:S(2)}) collective-permute-start(f32[3,8,128]{2,1,0:T(8,128)S(1)} %merge.1.after.mine), channel_id=1, source_target_pairs={{0,3},{1,2},{2,1},{3,0},{4,7},{5,6},{6,5},{7,4},{8,11},{9,10},{10,... | collective-permute-start | bytes 36872 | tf_op jit(solution)/shard_map/ppermute | solution.py:291

commit v10 on v9

--- a/solution.py
+++ b/solution.py
@@ -173,33 +173,36 @@
     return (lax.axis_index("seq_2") + lax.axis_index("seq_1")) % 2
 
 
-def merge_kernel(mine, theirs, out):
-    kept = out.shape[1]
+def merge_kernel(mine, theirs, own, sent):
+    kept = mine.shape[1] // 2
+    half = kept // 2
     rows = pl.ds(pl.multiple_of(half_kept() * kept, kept), kept)
-    both = joined(
-        [mine[i, rows, :] for i in range(3)], [theirs[i, rows, :] for i in range(3)]
-    )
+    both = joined([mine[i, rows, :] for i in range(3)], [theirs[i, rows, :] for i in range(3)])
+    odd = lax.axis_index("seq_1") % 2 == 1
     for i in range(3):
-        out[i] = both[i]
+        at = pl.ds(i * half, half)
+        own[at, :] = jnp.where(odd, both[i][half:], both[i][:half])
+        sent[at, :] = jnp.where(odd, both[i][:half], both[i][half:])
 
 
 def merge(mine, theirs):
+    shape = jax.ShapeDtypeStruct((3 * mine.shape[1] // 4, mine.shape[2]), jnp.float32)
     return pl.pallas_call(
         merge_kernel,
-        out_shape=jax.ShapeDtypeStruct((3, mine.shape[1] // 2, mine.shape[2]), jnp.float32),
+        out_shape=(shape, shape),
         in_specs=[VMEM, VMEM],
-        out_specs=VMEM,
+        out_specs=(VMEM, VMEM),
         compiler_params=PARAMS,
         name="merge",
     )(mine, theirs)
 
 
 def pack_kernel(mine, theirs, up_value, _, out):
-    head_dim = mine.shape[2]
-    accum, _, total = joined([mine[i] for i in range(3)], [theirs[i] for i in range(3)])
+    head_dim = mine.shape[1]
+    half = mine.shape[0] // 3
+    parts = [pl.ds(i * half, half) for i in range(3)]
+    accum, _, total = joined([mine[p, :] for p in parts], [theirs[p, :] for p in parts])
     mean = accum / total
-    half = mean.shape[0] // 2
-    mean = jnp.where(lax.axis_index("seq_1") % 2 == 1, mean[half:], mean[:half])
     value_map = up_value[lax.axis_index("grp")]
     value_map = jnp.where(
         half_kept() == 1, value_map[:, head_dim:], value_map[:, :head_dim]
@@ -296,9 +299,9 @@
     block_len = latent.shape[2]
     batch, q_heads, _ = queries.shape
     part, lat = attend(latent[0], up_key, queries, lengths, 2)
-    part = merge(part, swap(part, "seq_2", 1))
+    part, sent = merge(part, swap(part, "seq_2", 1))
     outgoing = slot(block_dest, lat, part, 8)
-    outgoing = pack(part, swap(part, ("seq_1", "seq_2"), 3), up_value, outgoing)
+    outgoing = pack(part, swap(sent, ("seq_1", "seq_2"), 3), up_value, outgoing)
     received = lax.all_to_all(outgoing, EXCHANGE, split_axis=0, concat_axis=0, tiled=True)
     decode, attended = unpack(received, groups, batch, q_heads, block_len)
     return (decode.reshape(1, groups, -1, *latent.shape[2:]), attended)

time: 51.9 us -> 51.8 us (level)
  no operation moved by 1% of the time
where the time goes in v10:
time: 51.8 us; the launch traced here: 51.4 us
  blocking collectives  42.3 us (82%)
  Pallas kernels  5.17 us (10%)
  starting transfers between devices  1.63 us (3%)
  waiting for transfers between devices  1.61 us (3%)
  between operations  0.68 us (1%)
    all_to_all x1, blocking collectives, body(): lax.all_to_all(outgoing, EXCHANGE, split_axis=0, concat_axis=0, tiled=True)  42.3 us
    pallas_call x1, Pallas kernels, attend(): pl.pallas_call(attend_kernel, out_shape=(jax.ShapeDtypeStruct((3, heads,...  2.23 us
    ppermute x2, starting transfers between devices, swap(): lax.ppermute(x, axes, [(i, i ^ mask) for i in range(lax.axis_size(axes))])  1.63 us
    ppermute x2, waiting for transfers between devices, swap(): lax.ppermute(x, axes, [(i, i ^ mask) for i in range(lax.axis_size(axes))])  1.61 us
    pallas_call x1, Pallas kernels, unpack(): pl.pallas_call(unpack_kernel, out_shape=(jax.ShapeDtypeStruct((1, groups,...  1.55 us
    pallas_call x1, Pallas kernels, slot(): pl.pallas_call(slot_kernel, out_shape=jax.ShapeDtypeStruct((count, 2 * bl...  1.18 us
  transfers between devices with their start and end apart: 2, of which 2 were waited for; matrix products, arithmetic and copies ran while one was open for 0% of the time, Pallas kernels for 2%

profile of v10, /device:TPU:0, one launch (start us, length us, event | category | flops | bytes accessed | tf_op | source)
XLA Modules:
  0.0 51.4 jit_solution(10254685418870501139)
XLA Ops:
  0.6 2.2 %attend.1 = (f32[3,16,128]{2,1,0:T(8,128)S(1)}, bf16[128,32,256]{2,1,0:T(8,128)(2,1)S(1)}) custom-call(s32[8]{0:T(128)} %ends.1, bf16[128,32,256]{2,1,0:T(8,128)(2,1)} %bitcast.4, bf16[4,128,256]{2,1,0:T(8,128)(2,1)} %up_key.1, bf16[8,64,128]{2,1,0:T(8,128)(2,1)} %queries.1), custom_call_target="tpu_custom_call" | custom-call | tf_op jit(solution)/shard_map/attend/pallas_call | solution.py:114
  2.9 0.0 copy-start
  2.9 0.1 collective-permute-start
  3.0 1.2 %collective-permute-done.theirs = f32[3,16,128]{2,1,0:T(8,128)S(1)} collective-permute-done((f32[3,16,128]{2,1,0:T(8,128)S(1)}, f32[3,16,128]{2,1,0:T(8,128)S(1)}, u32[]{:S(2)}, u32[]{:S(2)}) %collective-permute-start) | collective-permute-done | bytes 24608 | tf_op jit(solution)/shard_map/ppermute | solution.py:294
  4.2 1.5 %collective-permute-start.1 = (f32[12,128]{1,0:T(8,128)S(1)}, f32[12,128]{1,0:T(8,128)S(1)}, u32[]{:S(2)}, u32[]{:S(2)}) collective-permute-start(f32[12,128]{1,0:T(8,128)S(1)} %get-tuple-element.10), channel_id=1, source_target_pairs={{0,3},{1,2},{2,1},{3,0},{4,7},{5,6},{6,5},{7,4},{8,11},{9,10},{10,... | collective-permute-start | bytes 18440 | tf_op jit(solution)/shard_map/ppermute | solution.py:294
  5.7 1.2 %slot.1._ = bf16[128,72,128]{2,1,0:T(8,128)(2,1)S(1)} custom-call(s32[4096]{0:T(1024)} %dests.1, bf16[128,32,256]{2,1,0:T(8,128)(2,1)S(1)} %get-tuple-element.11.lat, f32[12,128]{1,0:T(8,128)S(1)} %get-tuple-element.9.after.mine), custom_call_target="tpu_custom_call" | custom-call | tf_op jit(solution)/shard_map/slot/pallas_call | solution.py:153
  6.9 0.4 collective-permute-done.1.theirs
  7.3 0.0 copy-done
  7.3 0.2 pack.1
  7.5 42.3 %all_to_all.5 = bf16[128,72,128]{2,1,0:T(8,128)(2,1)S(1)} all-to-all(bf16[128,72,128]{2,1,0:T(8,128)(2,1)S(1)} %pack.1), channel_id=1, replica_groups=mesh['grp'=4,'seq_0'=4,'seq_1'=4,'seq_2'=2] {'seq_2','grp','seq_1','seq_0'}, dimensions={0} | all-to-all | bytes 4718592 | tf_op jit(solution)/shard_map/all_to_all | solution.py:305
  49.9 1.6 %unpack.1 = (bf16[1,4,4,4,2,32,256]{6,5,4,3,2,1,0:T(8,128)(2,1)}, f32[8,8192]{1,0:T(8,128)}) custom-call(bf16[2,4,4,4,72,128]{5,4,3,2,1,0:T(8,128)(2,1)S(1)} %bitcast.3), custom_call_target="tpu_custom_call" | custom-call | tf_op jit(solution)/shard_map/unpack/pallas_call | solution.py:273
  (1 shorter events, 0.0 us)
Async XLA Ops:
  2.9 4.5 %copy-start = (bf16[4,128,256]{2,1,0:T(8,128)(2,1)S(1)}, bf16[4,128,256]{2,1,0:T(8,128)(2,1)}, u32[]{:S(2)}) copy-start(bf16[4,128,256]{2,1,0:T(8,128)(2,1)} %up_value.1) | copy-start | bytes 786436
  2.9 1.3 %collective-permute-start = (f32[3,16,128]{2,1,0:T(8,128)S(1)}, f32[3,16,128]{2,1,0:T(8,128)S(1)}, u32[]{:S(2)}, u32[]{:S(2)}) collective-permute-start(f32[3,16,128]{2,1,0:T(8,128)S(1)} %get-tuple-element.8.mine), channel_id=1, source_target_pairs={{0,1},{1,0},{2,3},{3,2},{4,5},{5,4},{6,7},{7,6},{8,9},{9,8},{10,11... | collective-permute-start | bytes 73736 | tf_op jit(solution)/shard_map/ppermute | solution.py:294
  4.2 3.2 %collective-permute-start.1 = (f32[12,128]{1,0:T(8,128)S(1)}, f32[12,128]{1,0:T(8,128)S(1)}, u32[]{:S(2)}, u32[]{:S(2)}) collective-permute-start(f32[12,128]{1,0:T(8,128)S(1)} %get-tuple-element.10), channel_id=1, source_target_pairs={{0,3},{1,2},{2,1},{3,0},{4,7},{5,6},{6,5},{7,4},{8,11},{9,10},{10,... | collective-permute-start | bytes 18440 | tf_op jit(solution)/shard_map/ppermute | solution.py:294

commit v11 on v9

--- a/solution.py
+++ b/solution.py
@@ -134,31 +134,44 @@
     return pltpu.with_memory_space_constraint(x, pltpu.HBM)
 
 
-def slot_kernel(dests, lat, after, outgoing, table, sem):
+def slot_kernel(dests, lat, up_value, after, outgoing, value_map, table, sems):
     count, block_len, width = lat.shape
     rank = width // 2
     first = pl.multiple_of(lax.axis_index(SEQ) * count, count)
-    copy = pltpu.make_async_copy(dests.at[pl.ds(first, count)], table, sem)
-    copy.start()
-    copy.wait()
+    left = pl.multiple_of(half_kept() * value_map.shape[1], value_map.shape[1])
+    copies = [
+        pltpu.make_async_copy(dests.at[pl.ds(first, count)], table, sems.at[0]),
+        pltpu.make_async_copy(
+            up_value.at[lax.axis_index("grp"), :, pl.ds(left, value_map.shape[1])],
+            value_map,
+            sems.at[1],
+        ),
+    ]
+    for copy in copies:
+        copy.start()
+    copies[0].wait()
     for b in range(count):
         d = table[b]
         to = (d & 1) * 64 + (d >> 5) * 16 + ((d >> 1) & 3) * 4 + ((d >> 3) & 3)
         outgoing[to, :block_len, :] = lat[b, :, :rank]
         outgoing[to, block_len : 2 * block_len, :] = lat[b, :, rank:]
-
-
-def slot(block_dest, lat, after, extra):
+    copies[1].wait()
+
+
+def slot(block_dest, lat, up_value, after, extra):
     count, block_len, width = lat.shape
     return pl.pallas_call(
         slot_kernel,
-        out_shape=jax.ShapeDtypeStruct((count, 2 * block_len + extra, width // 2), lat.dtype),
-        in_specs=[HBM, VMEM, VMEM],
-        out_specs=VMEM,
-        scratch_shapes=[pltpu.SMEM((count,), jnp.int32), pltpu.SemaphoreType.DMA],
+        out_shape=(
+            jax.ShapeDtypeStruct((count, 2 * block_len + extra, width // 2), lat.dtype),
+            jax.ShapeDtypeStruct((up_value.shape[1], up_value.shape[2] // 2), up_value.dtype),
+        ),
+        in_specs=[HBM, VMEM, HBM, VMEM],
+        out_specs=(VMEM, VMEM),
+        scratch_shapes=[pltpu.SMEM((count,), jnp.int32), pltpu.SemaphoreType.DMA((2,))],
         compiler_params=PARAMS,
         name="slot",
-    )(in_hbm(block_dest), lat, after)
+    )(in_hbm(block_dest), lat, in_hbm(up_value), after)
 
 
 def joined(first, second):
@@ -194,18 +207,13 @@
     )(mine, theirs)
 
 
-def pack_kernel(mine, theirs, up_value, _, out):
-    head_dim = mine.shape[2]
+def pack_kernel(mine, theirs, value_map, _, out):
     accum, _, total = joined([mine[i] for i in range(3)], [theirs[i] for i in range(3)])
     mean = accum / total
     half = mean.shape[0] // 2
     mean = jnp.where(lax.axis_index("seq_1") % 2 == 1, mean[half:], mean[:half])
-    value_map = up_value[lax.axis_index("grp")]
-    value_map = jnp.where(
-        half_kept() == 1, value_map[:, head_dim:], value_map[:, :head_dim]
-    )
     wide = lax.dot_general(
-        split(mean, 3), value_map, (((1,), (0,)), ((), ())), preferred_element_type=jnp.float32
+        split(mean, 3), value_map[...], (((1,), (0,)), ((), ())), preferred_element_type=jnp.float32
     )
     extra = split(wide[2 * half :] + wide[half : 2 * half] + wide[:half], 2)
     rows = out.shape[1] - extra.shape[0]
@@ -213,7 +221,7 @@
         out[b, rows:, :] = extra
 
 
-def pack(mine, theirs, up_value, outgoing):
+def pack(mine, theirs, value_map, outgoing):
     return pl.pallas_call(
         pack_kernel,
         out_shape=jax.ShapeDtypeStruct(outgoing.shape, outgoing.dtype),
@@ -222,7 +230,7 @@
         input_output_aliases={3: 0},
         compiler_params=PARAMS,
         name="pack",
-    )(mine, theirs, up_value, pltpu.with_memory_space_constraint(outgoing, pltpu.VMEM))
+    )(mine, theirs, value_map, pltpu.with_memory_space_constraint(outgoing, pltpu.VMEM))
 
 
 def unpack_kernel(received, decode, attended, rows_out, sems, row_sems):
@@ -297,8 +305,8 @@
     batch, q_heads, _ = queries.shape
     part, lat = attend(latent[0], up_key, queries, lengths, 2)
     part = merge(part, swap(part, "seq_2", 1))
-    outgoing = slot(block_dest, lat, part, 8)
-    outgoing = pack(part, swap(part, ("seq_1", "seq_2"), 3), up_value, outgoing)
+    outgoing, value_map = slot(block_dest, lat, up_value, part, 8)
+    outgoing = pack(part, swap(part, ("seq_1", "seq_2"), 3), value_map, outgoing)
     received = lax.all_to_all(outgoing, EXCHANGE, split_axis=0, concat_axis=0, tiled=True)
     decode, attended = unpack(received, groups, batch, q_heads, block_len)
     return (decode.reshape(1, groups, -1, *latent.shape[2:]), attended)

time: 51.9 us -> 51.9 us (level)
  no operation moved by 1% of the time
where the time goes in v11:
time: 51.9 us; the launch traced here: 51.4 us
  blocking collectives  42.3 us (82%)
  Pallas kernels  5.17 us (10%)
  waiting for transfers between devices  1.69 us (3%)
  starting transfers between devices  1.58 us (3%)
  between operations  0.67 us (1%)
    all_to_all x1, blocking collectives, body(): lax.all_to_all(outgoing, EXCHANGE, split_axis=0, concat_axis=0, tiled=True)  42.3 us
    pallas_call x1, Pallas kernels, attend(): pl.pallas_call(attend_kernel, out_shape=(jax.ShapeDtypeStruct((3, heads,...  2.23 us
    ppermute x2, waiting for transfers between devices, swap(): lax.ppermute(x, axes, [(i, i ^ mask) for i in range(lax.axis_size(axes))])  1.69 us
    ppermute x2, starting transfers between devices, swap(): lax.ppermute(x, axes, [(i, i ^ mask) for i in range(lax.axis_size(axes))])  1.58 us
    pallas_call x1, Pallas kernels, unpack(): pl.pallas_call(unpack_kernel, out_shape=(jax.ShapeDtypeStruct((1, groups,...  1.55 us
    pallas_call x1, Pallas kernels, slot(): pl.pallas_call(slot_kernel, out_shape=(jax.ShapeDtypeStruct((count, 2 * b...  1.19 us
  transfers between devices with their start and end apart: 2, of which 2 were waited for; matrix products, arithmetic and copies ran while one was open for 0% of the time, Pallas kernels for 2%

profile of v11, /device:TPU:0, one launch (start us, length us, event | category | flops | bytes accessed | tf_op | source)
XLA Modules:
  0.0 51.4 jit_solution(1983803348006305734)
XLA Ops:
  0.6 2.2 %attend.1 = (f32[3,16,128]{2,1,0:T(8,128)S(1)}, bf16[128,32,256]{2,1,0:T(8,128)(2,1)S(1)}) custom-call(s32[8]{0:T(128)} %ends.1, bf16[128,32,256]{2,1,0:T(8,128)(2,1)} %bitcast.4, bf16[4,128,256]{2,1,0:T(8,128)(2,1)} %up_key.1, bf16[8,64,128]{2,1,0:T(8,128)(2,1)} %queries.1), custom_call_target="tpu_custom_call" | custom-call | tf_op jit(solution)/shard_map/attend/pallas_call | solution.py:114
  2.9 0.1 collective-permute-start
  3.0 1.2 %collective-permute-done.theirs = f32[3,16,128]{2,1,0:T(8,128)S(1)} collective-permute-done((f32[3,16,128]{2,1,0:T(8,128)S(1)}, f32[3,16,128]{2,1,0:T(8,128)S(1)}, u32[]{:S(2)}, u32[]{:S(2)}) %collective-permute-start) | collective-permute-done | bytes 24608 | tf_op jit(solution)/shard_map/ppermute | solution.py:299
  4.2 1.5 %collective-permute-start.1 = (f32[3,8,128]{2,1,0:T(8,128)S(1)}, f32[3,8,128]{2,1,0:T(8,128)S(1)}, u32[]{:S(2)}, u32[]{:S(2)}) collective-permute-start(f32[3,8,128]{2,1,0:T(8,128)S(1)} %merge.1.after.mine), channel_id=1, source_target_pairs={{0,3},{1,2},{2,1},{3,0},{4,7},{5,6},{6,5},{7,4},{8,11},{9,10},{10,... | collective-permute-start | bytes 36872 | tf_op jit(solution)/shard_map/ppermute | solution.py:299
  5.7 1.2 %slot.1 = (bf16[128,72,128]{2,1,0:T(8,128)(2,1)S(1)}, bf16[128,128]{1,0:T(8,128)(2,1)S(1)}) custom-call(s32[4096]{0:T(1024)} %dests.1, bf16[128,32,256]{2,1,0:T(8,128)(2,1)S(1)} %get-tuple-element.9.lat, bf16[4,128,256]{2,1,0:T(8,128)(2,1)} %up_value.1, f32[3,8,128]{2,1,0:T(8,128)S(1)} %merge.1.after.mine), custom_call_target="tpu_custom_call" | custom-call | tf_op jit(solution)/shard_map/slot/pallas_call | solution.py:163
  6.9 0.5 collective-permute-done.1.theirs
  7.4 0.2 pack.1
  7.5 42.3 %all_to_all.5 = bf16[128,72,128]{2,1,0:T(8,128)(2,1)S(1)} all-to-all(bf16[128,72,128]{2,1,0:T(8,128)(2,1)S(1)} %pack.1), channel_id=1, replica_groups=mesh['grp'=4,'seq_0'=4,'seq_1'=4,'seq_2'=2] {'seq_2','grp','seq_1','seq_0'}, dimensions={0} | all-to-all | bytes 4718592 | tf_op jit(solution)/shard_map/all_to_all | solution.py:310
  49.9 1.6 %unpack.1 = (bf16[1,4,4,4,2,32,256]{6,5,4,3,2,1,0:T(8,128)(2,1)}, f32[8,8192]{1,0:T(8,128)}) custom-call(bf16[2,4,4,4,72,128]{5,4,3,2,1,0:T(8,128)(2,1)S(1)} %bitcast.3), custom_call_target="tpu_custom_call" | custom-call | tf_op jit(solution)/shard_map/unpack/pallas_call | solution.py:278
  (1 shorter events, 0.0 us)
Async XLA Ops:
  2.9 1.3 %collective-permute-start = (f32[3,16,128]{2,1,0:T(8,128)S(1)}, f32[3,16,128]{2,1,0:T(8,128)S(1)}, u32[]{:S(2)}, u32[]{:S(2)}) collective-permute-start(f32[3,16,128]{2,1,0:T(8,128)S(1)} %get-tuple-element.8.mine), channel_id=1, source_target_pairs={{0,1},{1,0},{2,3},{3,2},{4,5},{5,4},{6,7},{7,6},{8,9},{9,8},{10,11... | collective-permute-start | bytes 73736 | tf_op jit(solution)/shard_map/ppermute | solution.py:299
  4.2 3.2 %collective-permute-start.1 = (f32[3,8,128]{2,1,0:T(8,128)S(1)}, f32[3,8,128]{2,1,0:T(8,128)S(1)}, u32[]{:S(2)}, u32[]{:S(2)}) collective-permute-start(f32[3,8,128]{2,1,0:T(8,128)S(1)} %merge.1.after.mine), channel_id=1, source_target_pairs={{0,3},{1,2},{2,1},{3,0},{4,7},{5,6},{6,5},{7,4},{8,11},{9,10},{10,... | collective-permute-start | bytes 36872 | tf_op jit(solution)/shard_map/ppermute | solution.py:299

commit v12 on v11

--- a/solution.py
+++ b/solution.py
@@ -186,32 +186,35 @@
     return (lax.axis_index("seq_2") + lax.axis_index("seq_1")) % 2
 
 
-def merge_kernel(mine, theirs, out):
-    kept = out.shape[1]
+def merge_kernel(mine, theirs, own, sent):
+    kept = mine.shape[1] // 2
+    half = kept // 2
     rows = pl.ds(pl.multiple_of(half_kept() * kept, kept), kept)
-    both = joined(
-        [mine[i, rows, :] for i in range(3)], [theirs[i, rows, :] for i in range(3)]
-    )
+    both = joined([mine[i, rows, :] for i in range(3)], [theirs[i, rows, :] for i in range(3)])
+    odd = lax.axis_index("seq_1") % 2 == 1
     for i in range(3):
-        out[i] = both[i]
+        at = pl.ds(i * half, half)
+        own[at, :] = jnp.where(odd, both[i][half:], both[i][:half])
+        sent[at, :] = jnp.where(odd, both[i][:half], both[i][half:])
 
 
 def merge(mine, theirs):
+    shape = jax.ShapeDtypeStruct((3 * mine.shape[1] // 4, mine.shape[2]), jnp.float32)
     return pl.pallas_call(
         merge_kernel,
-        out_shape=jax.ShapeDtypeStruct((3, mine.shape[1] // 2, mine.shape[2]), jnp.float32),
+        out_shape=(shape, shape),
         in_specs=[VMEM, VMEM],
-        out_specs=VMEM,
+        out_specs=(VMEM, VMEM),
         compiler_params=PARAMS,
         name="merge",
     )(mine, theirs)
 
 
 def pack_kernel(mine, theirs, value_map, _, out):
-    accum, _, total = joined([mine[i] for i in range(3)], [theirs[i] for i in range(3)])
+    half = mine.shape[0] // 3
+    parts = [pl.ds(i * half, half) for i in range(3)]
+    accum, _, total = joined([mine[p, :] for p in parts], [theirs[p, :] for p in parts])
     mean = accum / total
-    half = mean.shape[0] // 2
-    mean = jnp.where(lax.axis_index("seq_1") % 2 == 1, mean[half:], mean[:half])
     wide = lax.dot_general(
         split(mean, 3), value_map[...], (((1,), (0,)), ((), ())), preferred_element_type=jnp.float32
     )
@@ -304,9 +307,9 @@
     block_len = latent.shape[2]
     batch, q_heads, _ = queries.shape
     part, lat = attend(latent[0], up_key, queries, lengths, 2)
-    part = merge(part, swap(part, "seq_2", 1))
+    part, sent = merge(part, swap(part, "seq_2", 1))
     outgoing, value_map = slot(block_dest, lat, up_value, part, 8)
-    outgoing = pack(part, swap(part, ("seq_1", "seq_2"), 3), value_map, outgoing)
+    outgoing = pack(part, swap(sent, ("seq_1", "seq_2"), 3), value_map, outgoing)
     received = lax.all_to_all(outgoing, EXCHANGE, split_axis=0, concat_axis=0, tiled=True)
     decode, attended = unpack(received, groups, batch, q_heads, block_len)
     return (decode.reshape(1, groups, -1, *latent.shape[2:]), attended)

time: 51.9 us -> 51.9 us (level)
  no operation moved by 1% of the time
where the time goes in v12:
time: 51.9 us; the launch traced here: 51.4 us
  blocking collectives  42.3 us (82%)
  Pallas kernels  5.17 us (10%)
  starting transfers between devices  1.63 us (3%)
  waiting for transfers between devices  1.6 us (3%)
  between operations  0.67 us (1%)
    all_to_all x1, blocking collectives, body(): lax.all_to_all(outgoing, EXCHANGE, split_axis=0, concat_axis=0, tiled=True)  42.3 us
    pallas_call x1, Pallas kernels, attend(): pl.pallas_call(attend_kernel, out_shape=(jax.ShapeDtypeStruct((3, heads,...  2.23 us
    ppermute x2, starting transfers between devices, swap(): lax.ppermute(x, axes, [(i, i ^ mask) for i in range(lax.axis_size(axes))])  1.63 us
    ppermute x2, waiting for transfers between devices, swap(): lax.ppermute(x, axes, [(i, i ^ mask) for i in range(lax.axis_size(axes))])  1.6 us
    pallas_call x1, Pallas kernels, unpack(): pl.pallas_call(unpack_kernel, out_shape=(jax.ShapeDtypeStruct((1, groups,...  1.55 us
    pallas_call x1, Pallas kernels, slot(): pl.pallas_call(slot_kernel, out_shape=(jax.ShapeDtypeStruct((count, 2 * b...  1.19 us
  transfers between devices with their start and end apart: 2, of which 2 were waited for; matrix products, arithmetic and copies ran while one was open for 0% of the time, Pallas kernels for 2%

profile of v12, /device:TPU:0, one launch (start us, length us, event | category | flops | bytes accessed | tf_op | source)
XLA Modules:
  0.0 51.4 jit_solution(17974859948043024388)
XLA Ops:
  0.6 2.2 %attend.1 = (f32[3,16,128]{2,1,0:T(8,128)S(1)}, bf16[128,32,256]{2,1,0:T(8,128)(2,1)S(1)}) custom-call(s32[8]{0:T(128)} %ends.1, bf16[128,32,256]{2,1,0:T(8,128)(2,1)} %bitcast.4, bf16[4,128,256]{2,1,0:T(8,128)(2,1)} %up_key.1, bf16[8,64,128]{2,1,0:T(8,128)(2,1)} %queries.1), custom_call_target="tpu_custom_call" | custom-call | tf_op jit(solution)/shard_map/attend/pallas_call | solution.py:114
  2.9 0.1 collective-permute-start
  3.0 1.2 %collective-permute-done.theirs = f32[3,16,128]{2,1,0:T(8,128)S(1)} collective-permute-done((f32[3,16,128]{2,1,0:T(8,128)S(1)}, f32[3,16,128]{2,1,0:T(8,128)S(1)}, u32[]{:S(2)}, u32[]{:S(2)}) %collective-permute-start) | collective-permute-done | bytes 24608 | tf_op jit(solution)/shard_map/ppermute | solution.py:302
  4.2 1.5 %collective-permute-start.1 = (f32[12,128]{1,0:T(8,128)S(1)}, f32[12,128]{1,0:T(8,128)S(1)}, u32[]{:S(2)}, u32[]{:S(2)}) collective-permute-start(f32[12,128]{1,0:T(8,128)S(1)} %get-tuple-element.12), channel_id=1, source_target_pairs={{0,3},{1,2},{2,1},{3,0},{4,7},{5,6},{6,5},{7,4},{8,11},{9,10},{10,... | collective-permute-start | bytes 18440 | tf_op jit(solution)/shard_map/ppermute | solution.py:302
  5.7 1.2 %slot.1 = (bf16[128,72,128]{2,1,0:T(8,128)(2,1)S(1)}, bf16[128,128]{1,0:T(8,128)(2,1)S(1)}) custom-call(s32[4096]{0:T(1024)} %dests.1, bf16[128,32,256]{2,1,0:T(8,128)(2,1)S(1)} %get-tuple-element.13.lat, bf16[4,128,256]{2,1,0:T(8,128)(2,1)} %up_value.1, f32[12,128]{1,0:T(8,128)S(1)} %get-tuple-element.11.after.mine), custom_call_target="tpu_custom_call" | custom-call | tf_op jit(solution)/shard_map/slot/pallas_call | solution.py:163
  6.9 0.4 collective-permute-done.1.theirs
  7.3 0.2 pack.1
  7.5 42.3 %all_to_all.5 = bf16[128,72,128]{2,1,0:T(8,128)(2,1)S(1)} all-to-all(bf16[128,72,128]{2,1,0:T(8,128)(2,1)S(1)} %pack.1), channel_id=1, replica_groups=mesh['grp'=4,'seq_0'=4,'seq_1'=4,'seq_2'=2] {'seq_2','grp','seq_1','seq_0'}, dimensions={0} | all-to-all | bytes 4718592 | tf_op jit(solution)/shard_map/all_to_all | solution.py:313
  49.8 1.6 %unpack.1 = (bf16[1,4,4,4,2,32,256]{6,5,4,3,2,1,0:T(8,128)(2,1)}, f32[8,8192]{1,0:T(8,128)}) custom-call(bf16[2,4,4,4,72,128]{5,4,3,2,1,0:T(8,128)(2,1)S(1)} %bitcast.3), custom_call_target="tpu_custom_call" | custom-call | tf_op jit(solution)/shard_map/unpack/pallas_call | solution.py:281
  (1 shorter events, 0.0 us)
Async XLA Ops:
  2.9 1.3 %collective-permute-start = (f32[3,16,128]{2,1,0:T(8,128)S(1)}, f32[3,16,128]{2,1,0:T(8,128)S(1)}, u32[]{:S(2)}, u32[]{:S(2)}) collective-permute-start(f32[3,16,128]{2,1,0:T(8,128)S(1)} %get-tuple-element.10.mine), channel_id=1, source_target_pairs={{0,1},{1,0},{2,3},{3,2},{4,5},{5,4},{6,7},{7,6},{8,9},{9,8},{10,11... | collective-permute-start | bytes 73736 | tf_op jit(solution)/shard_map/ppermute | solution.py:302
  4.2 3.2 %collective-permute-start.1 = (f32[12,128]{1,0:T(8,128)S(1)}, f32[12,128]{1,0:T(8,128)S(1)}, u32[]{:S(2)}, u32[]{:S(2)}) collective-permute-start(f32[12,128]{1,0:T(8,128)S(1)} %get-tuple-element.12), channel_id=1, source_target_pairs={{0,3},{1,2},{2,1},{3,0},{4,7},{5,6},{6,5},{7,4},{8,11},{9,10},{10,... | collective-permute-start | bytes 18440 | tf_op jit(solution)/shard_map/ppermute | solution.py:302
